TPU v7x, 256 devices: a whole 4x4x8 slice. The times are simulated.
256 devices in a mesh: row: 32 (over z, x_hi, core), col: 8 (over y, x_lo).
Axes of the slice: x: 4 (x_hi: 2, x_lo: 2; x = x_hi * 2 + x_lo), y: 4, z: 8, core: 2. Of those that a mesh axis runs over, the one named last changes fastest.
Arguments:
- queries: bfloat16 [262144, 256], P(('row', 'col')), may hold values from -6 to 6
- documents: bfloat16 [8192, 256], P(('row', 'col')), may hold values from -6 to 6
- log_norms: float32 [262144], P(('row', 'col')), may hold values from 7 to 11
- weights: float32 [262144], P(('row', 'col')), may hold values from 1 to 10
- positives: int32 [262144], P(('row', 'col')), may hold values from 0 to 8191
Outputs:
- grad_queries: bfloat16 [262144, 256], P(('row', 'col'))
- grad_documents: bfloat16 [8192, 256], P(('row', 'col'))
- loss: float32 [], replicated
All inputs are finite; a program needn't handle non-finite values.
Results may differ from a plain program's by a relative error of at most 0.001.
The roundings to bfloat16 on the way count: a program that leaves them out, or rounds other values in their place, can miss the bound.
Values may be sent and summed in bfloat16 or wider, within the bound.
No kernel may reach another device: no remote copies, remote signals or barrier semaphores. Data moves between devices by JAX's collectives and lax.ppermute only.
A program may use at most 128 MiB of HBM per device.

v0:
```python
import functools
import math

import jax
import jax.numpy as jnp
from jax import lax
from jax.experimental import pallas as pl
from jax.experimental.pallas import tpu as pltpu
from jax.sharding import Mesh
from jax.sharding import PartitionSpec as P


AXES = ("z", "xh", "core", "y", "xl")
X = ("xh", "xl")
Y = ("y",)
F32 = jnp.float32
BF16 = jnp.bfloat16
LOG2E = math.log2(math.e)
QT = 256
SUB = 256
SIDES = (0, 1, -1, 2)
SIDES_IN_TURN = (0, -1, 2, 1)
VMEM_LIMIT = 16 << 20


def other_core(array):
    return lax.ppermute(array, "core", [(0, 1), (1, 0)])


def moved(array, axes, distance):
    if distance == 0:
        return array
    peers = lax.axis_size(axes)
    return lax.ppermute(array, axes, [(i, (i + distance) % peers) for i in range(peers)])


def kernel(sizes, side, split, *refs):
    n_x, n_y, n_z = sizes
    place_ref, xd_ref, yd_ref, off_ref, w_ref, pos_ref, *refs = refs
    nq = off_ref.shape[1]
    if side == SIDES_IN_TURN[0]:
        own_ref, other_ref, *refs = refs
    else:
        q_ref, qt_ref, gq_in, found_in, *refs = refs
    half = xd_ref.shape[0]
    nd = 2 * half
    outs = nd // split
    gd_refs, refs = refs[:outs], refs[outs:]
    gq_ref, found_ref, *refs = refs
    if side == SIDES_IN_TURN[0]:
        q_ref, qt_ref, *refs = refs
    dt_ref, id_ref, c_ref, gd_ref, sems = refs

    if side == SIDES_IN_TURN[0]:
        for i, ref in enumerate((own_ref, other_ref)):
            part = slice(i * (nq // 2), (i + 1) * (nq // 2))
            q_ref[part, :] = ref[...]
            qt_ref[:, part] = ref[...].T
    gd_ref[...] = jnp.zeros(gd_ref.shape, F32)
    piece = half // (4 * n_z // 2)
    x, y, core = place_ref[0], place_ref[1], place_ref[2]
    row = lax.broadcasted_iota(jnp.int32, (piece, 128), 0)
    for block in range(nd // piece):
        group, rest_of = divmod(block, half // piece)
        step, z = divmod(rest_of, n_z // 2)
        dx, dy = (side, SIDES[step]) if group == 0 else (SIDES[step], side)
        from_x = (x - dx + n_x) % n_x
        from_y = (y - dy + n_y) % n_y
        base = (((z + group * (n_z // 2)) * 2 + from_x // 2) * 2 + core) * 2 * n_y + from_y * 2 + from_x % 2
        id_ref[block * piece : (block + 1) * piece, :] = row + base * piece
    for i, ref in enumerate((xd_ref, yd_ref)):
        dt_ref[:, i * half : (i + 1) * half] = ref[...].T

    def front(tile, slot):
        cols = pl.ds(pl.multiple_of(tile * QT, QT), QT)
        q_t = qt_ref[:, cols]
        off = off_ref[:, cols]
        w = w_ref[:, cols]
        pos = pos_ref[:, cols]
        found = jnp.zeros((8, QT), F32)
        for r in range(0, nd, SUB):
            rows = slice(r, r + SUB)
            docs = (xd_ref, yd_ref)[r // half][r % half : r % half + SUB, :]
            scores = jnp.dot(docs, q_t, preferred_element_type=F32)
            probs = jnp.exp2(scores * (0.0625 * LOG2E) - off)
            hits = jnp.concatenate([id_ref[rows, :]] * (QT // 128), 1) == pos
            c_ref[slot, rows, :] = (probs - jnp.where(hits, w, 0.0)).astype(BF16)
            found = found + jnp.sum(jnp.where(hits, scores, 0.0).reshape(SUB // 8, 8, QT), 0)
        found_ref[:, cols] = found if side == SIDES_IN_TURN[0] else found_in[:, cols] + found

    def back(tile, slot):
        cols = pl.ds(pl.multiple_of(tile * QT, QT), QT)
        q = q_ref[cols, :]
        for r in range(0, nd, SUB):
            gd_ref[r : r + SUB, :] += jnp.dot(c_ref[slot, r : r + SUB, :], q, preferred_element_type=F32)
        term = jnp.dot(dt_ref[...], c_ref[slot], preferred_element_type=F32)
        gq_ref[:, cols] = term if side == SIDES_IN_TURN[0] else gq_in[:, cols] + term

    tiles = nq // QT
    front(0, 0)

    def pair(i, _):
        front(2 * i + 1, 1)
        back(2 * i, 0)
        front((2 * i + 2) % tiles, 0)
        back(2 * i + 1, 1)
        return 0

    lax.fori_loop(0, tiles // 2, pair, 0)
    leave = [
        pltpu.make_async_copy(gd_ref.at[pl.ds(i * split, split)], gd_refs[i], sems.at[i]) for i in range(outs)
    ]
    for copy in leave:
        copy.start()
    for copy in leave:
        copy.wait()


def fused(side, split, place, x_docs, y_docs, off, w, pos, extra, sizes):
    nq = off.shape[1]
    width = x_docs.shape[1]
    nd = 2 * x_docs.shape[0]
    vmem = pl.BlockSpec(memory_space=pltpu.VMEM)
    hbm = pl.BlockSpec(memory_space=pltpu.HBM)
    first = side == SIDES_IN_TURN[0]
    operands = [place, x_docs, y_docs, off, w, pos, *extra]
    outs = nd // split
    out_shape = [pltpu.HBM((split, width), F32)] * outs
    out_shape += [jax.ShapeDtypeStruct((width, nq), F32), jax.ShapeDtypeStruct((8, nq), F32)]
    if first:
        out_shape += [jax.ShapeDtypeStruct((nq, width), BF16), jax.ShapeDtypeStruct((width, nq), BF16)]
    return pl.pallas_call(
        functools.partial(kernel, sizes, side, split),
        in_specs=[pl.BlockSpec(memory_space=pltpu.SMEM)] + [vmem] * (len(operands) - 1),
        out_specs=[hbm] * outs + [vmem] * (len(out_shape) - outs),
        out_shape=out_shape,
        scratch_shapes=[
            pltpu.VMEM((width, nd), BF16),
            pltpu.VMEM((nd, 128), jnp.int32),
            pltpu.VMEM((2, nd, QT), BF16),
            pltpu.VMEM((nd, width), F32),
            pltpu.SemaphoreType.DMA((outs,)),
        ],
        input_output_aliases={} if first else {8: outs},
        compiler_params=pltpu.CompilerParams(vmem_limit_bytes=VMEM_LIMIT),
        cost_estimate=pl.CostEstimate(flops=6 * nq * nd * width, bytes_accessed=8 << 20, transcendentals=nq * nd),
        name="fused",
    )(*operands)


def all_sides(array, axes):
    return {side: moved(array, axes, side) for side in (0, 2, 1, -1)}


def on_device(queries, documents, log_norms, weights, positives):
    own, width = queries.shape
    piece = documents.shape[0]
    total_q = own * lax.axis_size(AXES)
    n_x, n_y, n_z = lax.axis_size(X), lax.axis_size(Y), lax.axis_size("z")
    place = jnp.stack([lax.axis_index(X), lax.axis_index(Y), lax.axis_index("core")]).astype(jnp.int32)

    rows = jnp.stack([log_norms, weights, positives.astype(F32)])
    rows = jnp.concatenate([rows, other_core(rows)], 1)
    other_queries = other_core(queries)
    w = rows[1:2]
    off = rows[0:1] * LOG2E - jnp.log2(w)
    pos = rows[2:3].astype(jnp.int32)

    column = lax.all_to_all(jnp.broadcast_to(documents[None], (n_z, piece, width)), "z", 0, 0, tiled=True)
    x_part, y_part = column.reshape(2, n_z // 2 * piece, width)
    x_near = all_sides(x_part, Y)
    y_near = all_sides(y_part, X)
    x_docs = all_sides(jnp.concatenate([x_near[s] for s in SIDES]), X)
    y_docs = all_sides(jnp.concatenate([y_near[s] for s in SIDES]), Y)

    half = x_docs[0].shape[0]
    terms = {}
    extra = (queries, other_queries)
    for side in SIDES_IN_TURN:
        split = half // 2 if side == 2 else half
        outs = 2 * half // split
        got = fused(side, split, place, x_docs[side], y_docs[side], off, w, pos, extra, (n_x, n_y, n_z))
        terms[side] = got[:outs]
        grad_q, found = got[outs : outs + 2]
        layouts = got[outs + 2 :] or layouts
        extra = (*layouts, grad_q, found)

    ends = (weights * log_norms).reshape(-1, width).sum(0)
    lost = -0.0625 * (w * found).reshape(8, -1, width).sum(1)
    lost = lost.at[0].add(ends)
    lost = lost + other_core(lost)

    def ring(own_term, ahead, behind, far_a, far_b, axes):
        n = half // 2
        tail = lost if axes == X else None
        far_a = moved(far_a, axes, -1)
        far_b = moved(far_b, axes, 1)
        ahead = jnp.concatenate([ahead[:n] + far_a, ahead[n:], *([] if tail is None else [tail])])
        behind = jnp.concatenate([behind[:n], behind[n:] + far_b, *([] if tail is None else [tail])])
        ahead, behind = moved(ahead, axes, -1), moved(behind, axes, 1)
        total = own_term + ahead[:half] + behind[:half]
        return (total, None) if tail is None else (total, tail + moved(tail, axes, 2) + ahead[half:] + behind[half:])

    x_total, x_lost = ring(terms[0][0], terms[1][0], terms[-1][0], terms[2][0], terms[2][1], X)
    y_total, _ = ring(terms[0][1], terms[1][1], terms[-1][1], terms[2][2], terms[2][3], Y)
    n = half // 4
    x_sum = sum(
        moved(jnp.concatenate([x_total[i * n : (i + 1) * n], x_lost]), Y, -s) for i, s in enumerate(SIDES)
    )
    y_sum = sum(moved(y_total[i * n : (i + 1) * n], X, -s) for i, s in enumerate(SIDES))
    part = jnp.concatenate([x_sum[:n], y_sum]).reshape(n_z, piece, width)
    part = jnp.concatenate([part, jnp.broadcast_to(x_sum[n:][None], (n_z, 8, width))], 1)
    part = lax.all_to_all(part, "z", 0, 0, tiled=True).sum(0)
    grad_documents = (part[:piece] * 0.0625).astype(BF16)
    loss = jnp.sum(part[piece:]) / total_q

    grad_q = grad_q[:, :own] + other_core(grad_q[:, own:])
    grad_queries = (grad_q.T * 0.0625).astype(BF16)
    return (grad_queries, grad_documents, loss)


def solution(mesh):
    torus = Mesh(mesh.devices.reshape(8, 2, 2, 4, 2), AXES)
    placed = (P(AXES, None), P(AXES, None), P(AXES), P(AXES), P(AXES))
    return jax.shard_map(
        on_device,
        mesh=torus,
        in_specs=placed,
        out_specs=(P(AXES, None), P(AXES, None), P()),
        check_vma=False,
    )
```

profile of v0, /device:TPU:32, one launch (start us, length us, event | category | flops | bytes accessed | tf_op | source)
XLA Modules:
  0.0 130.5 jit_solution(7055156898194141981)
XLA Ops:
  0.6 1.4 %broadcast_in_dim.4 = bf16[8,32,256]{2,1,0:T(8,128)(2,1)} broadcast(bf16[32,256]{1,0:T(8,128)(2,1)} %param.8), dimensions={1,2} | broadcast | bytes 147456 | tf_op jit(solution)/shard_map/broadcast_in_dim | solution.py:169
  2.0 8.6 %all-to-all-start = ((bf16[8,32,256]{2,1,0:T(8,128)(2,1)}), bf16[8,32,256]{2,1,0:T(8,128)(2,1)S(1)}, u32[]{:S(2)}, u32[]{:S(2)}) async-start(bf16[8,32,256]{2,1,0:T(8,128)(2,1)} %broadcast_in_dim.4), calls=%async_computation | async-start | bytes 262144 | tf_op jit(solution)/shard_map/all_to_all | solution.py:169
  10.6 0.7 convert_element_type.15
  11.3 0.7 pad_maximum_fusion.12
  12.6 0.7 mul.47
  13.4 4.6 %all-to-all-done = bf16[8,32,256]{2,1,0:T(8,128)(2,1)S(1)} async-done(((bf16[8,32,256]{2,1,0:T(8,128)(2,1)}), bf16[8,32,256]{2,1,0:T(8,128)(2,1)S(1)}, u32[]{:S(2)}, u32[]{:S(2)}) %all-to-all-start) | async-done | bytes 131104 | tf_op jit(solution)/shard_map/all_to_all | solution.py:169
  18.0 1.6 %collective-permute-start.4 = (bf16[128,256]{1,0:T(8,128)(2,1)S(1)}, bf16[128,256]{1,0:T(8,128)(2,1)S(1)}, u32[]{:S(2)}, u32[]{:S(2)}) collective-permute-start(bf16[128,256]{1,0:T(8,128)(2,1)S(1)} %bitcast.21), channel_id=1, source_target_pairs={{0,1},{1,16},{16,17},{17,0},{2,3},{3,18},{18,19},{19,2},{4,5},{5,2... | collective-permute-start | bytes 196616 | tf_op jit(solution)/shard_map/ppermute | solution.py:34
  19.6 1.7 %collective-permute-start.5 = (bf16[128,256]{1,0:T(8,128)(2,1)S(1)}, bf16[128,256]{1,0:T(8,128)(2,1)S(1)}, u32[]{:S(2)}, u32[]{:S(2)}) collective-permute-start(bf16[128,256]{1,0:T(8,128)(2,1)S(1)} %bitcast.22), channel_id=1, source_target_pairs={{0,17},{1,0},{16,1},{17,16},{2,19},{3,2},{18,3},{19,18},{4,21},{5,... | collective-permute-start | bytes 196616 | tf_op jit(solution)/shard_map/ppermute | solution.py:34
  21.4 1.8 %collective-permute-start.6 = (bf16[128,256]{1,0:T(8,128)(2,1)S(1)}, bf16[128,256]{1,0:T(8,128)(2,1)S(1)}, u32[]{:S(2)}, u32[]{:S(2)}) collective-permute-start(bf16[128,256]{1,0:T(8,128)(2,1)S(1)} %bitcast.23), channel_id=1, source_target_pairs={{0,16},{1,17},{16,0},{17,1},{2,18},{3,19},{18,2},{19,3},{4,20},{5,... | collective-permute-start | bytes 196616 | tf_op jit(solution)/shard_map/ppermute | solution.py:34
  23.2 0.9 fusion.8
  24.0 1.7 %collective-permute-start = (bf16[128,256]{1,0:T(8,128)(2,1)S(1)}, bf16[128,256]{1,0:T(8,128)(2,1)S(1)}, u32[]{:S(2)}, u32[]{:S(2)}) collective-permute-start(bf16[128,256]{1,0:T(8,128)(2,1)S(1)} %bitcast.17), channel_id=1, source_target_pairs={{0,2},{2,4},{4,6},{6,0},{1,3},{3,5},{5,7},{7,1},{8,10},{10,12},{12... | collective-permute-start | bytes 196616 | tf_op jit(solution)/shard_map/ppermute | solution.py:34
  25.7 1.7 %collective-permute-start.1 = (bf16[128,256]{1,0:T(8,128)(2,1)S(1)}, bf16[128,256]{1,0:T(8,128)(2,1)S(1)}, u32[]{:S(2)}, u32[]{:S(2)}) collective-permute-start(bf16[128,256]{1,0:T(8,128)(2,1)S(1)} %bitcast.18), channel_id=1, source_target_pairs={{0,6},{2,0},{4,2},{6,4},{1,7},{3,1},{5,3},{7,5},{8,14},{10,8},{12,... | collective-permute-start | bytes 196616 | tf_op jit(solution)/shard_map/ppermute | solution.py:34
  27.4 2.0 %collective-permute-start.2 = (bf16[128,256]{1,0:T(8,128)(2,1)S(1)}, bf16[128,256]{1,0:T(8,128)(2,1)S(1)}, u32[]{:S(2)}, u32[]{:S(2)}) collective-permute-start(bf16[128,256]{1,0:T(8,128)(2,1)S(1)} %bitcast.19), channel_id=1, source_target_pairs={{0,4},{2,6},{4,0},{6,2},{1,5},{3,7},{5,1},{7,3},{8,12},{10,14},{12... | collective-permute-start | bytes 196616 | tf_op jit(solution)/shard_map/ppermute | solution.py:34
  29.4 1.1 collective-permute-start.13
  30.5 1.7 %collective-permute-start.11 = (bf16[512,256]{1,0:T(8,128)(2,1)S(1)}, bf16[512,256]{1,0:T(8,128)(2,1)S(1)}, u32[]{:S(2)}, u32[]{:S(2)}) collective-permute-start(bf16[512,256]{1,0:T(8,128)(2,1)S(1)} %pad_maximum_fusion.10.refs_2_), channel_id=1, source_target_pairs={{0,4},{2,6},{4,0},{6,2},{1,5},{3,7},{5,1},{7,3},{8,12},{10,14},{12... | collective-permute-start | bytes 786440 | tf_op jit(solution)/shard_map/ppermute | solution.py:34
  32.2 1.6 %collective-permute-done.2 = bf16[128,256]{1,0:T(8,128)(2,1)S(1)} collective-permute-done((bf16[128,256]{1,0:T(8,128)(2,1)S(1)}, bf16[128,256]{1,0:T(8,128)(2,1)S(1)}, u32[]{:S(2)}, u32[]{:S(2)}) %collective-permute-start.2) | collective-permute-done | bytes 65568 | tf_op jit(solution)/shard_map/ppermute | solution.py:34
  33.9 1.2 collective-permute-start.12
  35.1 1.5 %collective-permute-start.10 = (bf16[512,256]{1,0:T(8,128)(2,1)S(1)}, bf16[512,256]{1,0:T(8,128)(2,1)S(1)}, u32[]{:S(2)}, u32[]{:S(2)}) collective-permute-start(bf16[512,256]{1,0:T(8,128)(2,1)S(1)} %pad_maximum_fusion.9.refs_1_), channel_id=1, source_target_pairs={{0,16},{1,17},{16,0},{17,1},{2,18},{3,19},{18,2},{19,3},{4,20},{5,... | collective-permute-start | bytes 786440 | tf_op jit(solution)/shard_map/ppermute | solution.py:34
  36.6 0.6 collective-permute-start.7
  37.2 1.0 copy-done
  38.3 6.9 %fused.4 = (f32[512,256]{1,0:T(8,128)}, f32[512,256]{1,0:T(8,128)}, f32[256,2048]{1,0:T(8,128)S(1)}, f32[8,2048]{1,0:T(8,128)S(1)}, bf16[2048,256]{1,0:T(8,128)(2,1)S(1)}, /*index=5*/bf16[256,2048]{1,0:T(8,128)(2,1)S(1)}) custom-call(s32[3]{0:T(128)S(1)} %pad_add_fusion.refs_0_, bf16[512,256]{1,0:T(8,128)(2,1)S(1)} %pad_maximum_fusion.9.refs_1_, ...), custom_call_target="tpu_custom_call" | custom-call | flops 3221225472 | bytes 8388608 | tf_op jit(solution)/shard_map/fused/pallas_call | solution.py:132
  45.2 0.7 collective-permute-start.3
  45.9 6.7 %fused.5 = (f32[512,256]{1,0:T(8,128)}, f32[512,256]{1,0:T(8,128)}, f32[256,2048]{1,0:T(8,128)S(1)}, f32[8,2048]{1,0:T(8,128)S(1)}) custom-call(s32[3]{0:T(128)S(1)} %pad_add_fusion.refs_0_, bf16[512,256]{1,0:T(8,128)(2,1)S(1)} %collective-permute-done.12.refs_1_, ...), custom_call_target="tpu_custom_call", output_to_operand_aliasing={{2}: (8, {})} | custom-call | flops 3221225472 | bytes 8388608 | tf_op jit(solution)/shard_map/fused/pallas_call | solution.py:132
  52.7 6.7 %fused.6 = (f32[256,256]{1,0:T(8,128)}, f32[256,256]{1,0:T(8,128)}, f32[256,256]{1,0:T(8,128)}, f32[256,256]{1,0:T(8,128)}, f32[256,2048]{1,0:T(8,128)S(1)}, /*index=5*/f32[8,2048]{1,0:T(8,128)S(1)}) custom-call(s32[3]{0:T(128)S(1)} %pad_add_fusion.refs_0_, bf16[512,256]{1,0:T(8,128)(2,1)S(1)} %collective-permute-done.10.refs_1_, ...), custom_call_target="tpu_custom_call", output_to_operand_aliasing={{4}: (8, {})} | custom-call | flops 3221225472 | bytes 8388608 | tf_op jit(solution)/shard_map/fused/pallas_call | solution.py:132
  59.4 2.7 %collective-permute-start.24 = (f32[256,256]{1,0:T(8,128)}, f32[256,256]{1,0:T(8,128)S(1)}, u32[]{:S(2)}, u32[]{:S(2)}) collective-permute-start(f32[256,256]{1,0:T(8,128)} %get-tuple-element.52), channel_id=1, source_target_pairs={{0,6},{2,0},{4,2},{6,4},{1,7},{3,1},{5,3},{7,5},{8,14},{10,8},{12,... | collective-permute-start | bytes 786440 | tf_op jit(solution)/shard_map/ppermute | solution.py:34
  62.1 6.7 %fused.7 = (f32[512,256]{1,0:T(8,128)}, f32[512,256]{1,0:T(8,128)}, f32[256,2048]{1,0:T(8,128)S(1)}, f32[8,2048]{1,0:T(8,128)S(1)}) custom-call(s32[3]{0:T(128)S(1)} %pad_add_fusion.refs_0_, bf16[512,256]{1,0:T(8,128)(2,1)S(1)} %collective-permute-done.3.refs_1_, ...), custom_call_target="tpu_custom_call", output_to_operand_aliasing={{2}: (8, {})} | custom-call | flops 3221225472 | bytes 8388608 | tf_op jit(solution)/shard_map/fused/pallas_call | solution.py:132
  69.2 1.6 %collective-permute-start.18 = (f32[256,256]{1,0:T(8,128)S(1)}, f32[256,256]{1,0:T(8,128)S(1)}, u32[]{:S(2)}, u32[]{:S(2)}) collective-permute-start(f32[256,256]{1,0:T(8,128)S(1)} %copy-done.7), channel_id=1, source_target_pairs={{0,1},{1,16},{16,17},{17,0},{2,3},{3,18},{18,19},{19,2},{4,5},{5,2... | collective-permute-start | bytes 786440 | tf_op jit(solution)/shard_map/ppermute | solution.py:34
  70.7 1.8 %collective-permute-start.15 = (f32[256,256]{1,0:T(8,128)S(1)}, f32[256,256]{1,0:T(8,128)S(1)}, u32[]{:S(2)}, u32[]{:S(2)}) collective-permute-start(f32[256,256]{1,0:T(8,128)S(1)} %copy-done.6), channel_id=1, source_target_pairs={{0,17},{1,0},{16,1},{17,16},{2,19},{3,2},{18,3},{19,18},{4,21},{5,... | collective-permute-start | bytes 786440 | tf_op jit(solution)/shard_map/ppermute | solution.py:34
  72.5 1.1 slice_add_fusion.3
  73.7 3.2 %collective-permute-start.25 = (f32[512,256]{1,0:T(8,128)S(1)}, f32[512,256]{1,0:T(8,128)S(1)}, u32[]{:S(2)}, u32[]{:S(2)}) collective-permute-start(f32[512,256]{1,0:T(8,128)S(1)} %pad_maximum_fusion.2), channel_id=1, source_target_pairs={{0,6},{2,0},{4,2},{6,4},{1,7},{3,1},{5,3},{7,5},{8,14},{10,8},{12,... | collective-permute-start | bytes 1572872 | tf_op jit(solution)/shard_map/ppermute | solution.py:34
  76.9 2.3 %collective-permute-done.26 = f32[256,256]{1,0:T(8,128)S(1)} collective-permute-done((f32[256,256]{1,0:T(8,128)}, f32[256,256]{1,0:T(8,128)S(1)}, u32[]{:S(2)}, u32[]{:S(2)}) %collective-permute-start.26) | collective-permute-done | bytes 262176 | tf_op jit(solution)/shard_map/ppermute | solution.py:34
  79.6 2.8 %collective-permute-start.17 = (f32[520,256]{1,0:T(8,128)S(1)}, f32[520,256]{1,0:T(8,128)S(1)}, u32[]{:S(2)}, u32[]{:S(2)}) collective-permute-start(f32[520,256]{1,0:T(8,128)S(1)} %get-tuple-element.84), channel_id=1, source_target_pairs={{0,17},{1,0},{16,1},{17,16},{2,19},{3,2},{18,3},{19,18},{4,21},{5,... | collective-permute-start | bytes 1597448 | tf_op jit(solution)/shard_map/ppermute | solution.py:34
  82.5 1.1 slice.110
  83.6 4.2 %collective-permute-done.25 = f32[512,256]{1,0:T(8,128)S(1)} collective-permute-done((f32[512,256]{1,0:T(8,128)S(1)}, f32[512,256]{1,0:T(8,128)S(1)}, u32[]{:S(2)}, u32[]{:S(2)}) %collective-permute-start.25) | collective-permute-done | bytes 524320 | tf_op jit(solution)/shard_map/ppermute | solution.py:34
  87.8 1.8 %collective-permute-start.20 = (f32[8,256]{1,0:T(8,128)S(1)}, f32[8,256]{1,0:T(8,128)S(1)}, u32[]{:S(2)}, u32[]{:S(2)}) collective-permute-start(f32[8,256]{1,0:T(8,128)S(1)} %add.71), channel_id=1, source_target_pairs={{0,16},{1,17},{16,0},{17,1},{2,18},{3,19},{18,2},{19,3},{4,20},{5,... | collective-permute-start | bytes 24584 | tf_op jit(solution)/shard_map/ppermute | solution.py:34
  89.6 4.3 %collective-permute-done.27 = f32[512,256]{1,0:T(8,128)S(1)} collective-permute-done((f32[512,256]{1,0:T(8,128)S(1)}, f32[512,256]{1,0:T(8,128)S(1)}, u32[]{:S(2)}, u32[]{:S(2)}) %collective-permute-start.27) | collective-permute-done | bytes 524320 | tf_op jit(solution)/shard_map/ppermute | solution.py:34
  94.1 2.8 %collective-permute-start.28 = (f32[128,256]{1,0:T(8,128)S(1)}, f32[128,256]{1,0:T(8,128)S(1)}, u32[]{:S(2)}, u32[]{:S(2)}) collective-permute-start(f32[128,256]{1,0:T(8,128)S(1)} %get-tuple-element.63), channel_id=1, source_target_pairs={{0,17},{1,0},{16,1},{17,16},{2,19},{3,2},{18,3},{19,18},{4,21},{5,... | collective-permute-start | bytes 393224 | tf_op jit(solution)/shard_map/ppermute | solution.py:34
  97.2 2.1 %collective-permute-start.30 = (f32[128,256]{1,0:T(8,128)S(1)}, f32[128,256]{1,0:T(8,128)S(1)}, u32[]{:S(2)}, u32[]{:S(2)}) collective-permute-start(f32[128,256]{1,0:T(8,128)S(1)} %get-tuple-element.64), channel_id=1, source_target_pairs={{0,16},{1,17},{16,0},{17,1},{2,18},{3,19},{18,2},{19,3},{4,20},{5,... | collective-permute-start | bytes 393224 | tf_op jit(solution)/shard_map/ppermute | solution.py:34
  99.5 3.9 %collective-permute-start.21 = (f32[136,256]{1,0:T(8,128)S(1)}, f32[136,256]{1,0:T(8,128)S(1)}, u32[]{:S(2)}, u32[]{:S(2)}) collective-permute-start(f32[136,256]{1,0:T(8,128)S(1)} %get-tuple-element.81), channel_id=1, source_target_pairs={{0,6},{2,0},{4,2},{6,4},{1,7},{3,1},{5,3},{7,5},{8,14},{10,8},{12,... | collective-permute-start | bytes 417800 | tf_op jit(solution)/shard_map/ppermute | solution.py:34
  103.4 1.4 %collective-permute-done.29 = f32[128,256]{1,0:T(8,128)S(1)} collective-permute-done((f32[128,256]{1,0:T(8,128)S(1)}, f32[128,256]{1,0:T(8,128)S(1)}, u32[]{:S(2)}, u32[]{:S(2)}) %collective-permute-start.29) | collective-permute-done | bytes 131104 | tf_op jit(solution)/shard_map/ppermute | solution.py:34
  105.0 1.6 %collective-permute-done.21 = f32[136,256]{1,0:T(8,128)S(1)} collective-permute-done((f32[136,256]{1,0:T(8,128)S(1)}, f32[136,256]{1,0:T(8,128)S(1)}, u32[]{:S(2)}, u32[]{:S(2)}) %collective-permute-start.21) | collective-permute-done | bytes 139296 | tf_op jit(solution)/shard_map/ppermute | solution.py:34
  106.6 5.2 %collective-permute-done.22 = f32[136,256]{1,0:T(8,128)S(1)} collective-permute-done((f32[136,256]{1,0:T(8,128)S(1)}, f32[136,256]{1,0:T(8,128)S(1)}, u32[]{:S(2)}, u32[]{:S(2)}) %collective-permute-start.22) | collective-permute-done | bytes 139296 | tf_op jit(solution)/shard_map/ppermute | solution.py:34
  111.9 0.8 pad_maximum_fusion.4
  112.7 5.0 %all-to-all-start.1 = ((f32[8,40,256]{2,1,0:T(8,128)}), f32[8,40,256]{2,1,0:T(8,128)S(1)}, u32[]{:S(2)}, u32[]{:S(2)}) async-start(f32[8,40,256]{2,1,0:T(8,128)} %pad_maximum_fusion.4), calls=%async_computation.1 | async-start | bytes 655360 | tf_op jit(solution)/shard_map/all_to_all | solution.py:213
  117.7 1.4 %fusion = bf16[1024,256]{0,1:T(8,128)(2,1)S(1)} fusion(f32[256,1024]{1,0:T(8,128)} %collective-permute-done.14, f32[256,2048]{1,0:T(8,128)S(1)} %get-tuple-element.43), kind=kLoop, calls=%fused_computation.3 | loop fusion | flops 786432 | bytes 2621440 | tf_op jit(solution)/shard_map/convert_element_type | solution.py:218
  119.1 1.0 copy.12
  120.1 7.3 %all-to-all-done.1 = f32[8,40,256]{2,1,0:T(8,128)S(1)} async-done(((f32[8,40,256]{2,1,0:T(8,128)}), f32[8,40,256]{2,1,0:T(8,128)S(1)}, u32[]{:S(2)}, u32[]{:S(2)}) %all-to-all-start.1) | async-done | bytes 327712 | tf_op jit(solution)/shard_map/all_to_all | solution.py:213
  127.5 0.6 fusion.6
  (81 shorter events, 2.9 us)
Async XLA Ops:
  2.0 16.0 %all-to-all-start = ((bf16[8,32,256]{2,1,0:T(8,128)(2,1)}), bf16[8,32,256]{2,1,0:T(8,128)(2,1)S(1)}, u32[]{:S(2)}, u32[]{:S(2)}) async-start(bf16[8,32,256]{2,1,0:T(8,128)(2,1)} %broadcast_in_dim.4), calls=%async_computation | async-start | bytes 262144 | tf_op jit(solution)/shard_map/all_to_all | solution.py:169
  12.0 11.2 %collective-permute-start.8 = (f32[3,1024]{1,0:T(4,128)S(1)}, f32[3,1024]{1,0:T(4,128)S(1)}, u32[]{:S(2)}, u32[]{:S(2)}) collective-permute-start(f32[3,1024]{1,0:T(4,128)S(1)} %pad_maximum_fusion.12), channel_id=1, source_target_pairs={{0,8},{8,0},{1,9},{9,1},{2,10},{10,2},{3,11},{11,3},{4,12},{12,4},... | collective-permute-start | bytes 36872 | tf_op jit(solution)/shard_map/ppermute | solution.py:27
  12.1 24.5 %collective-permute-start.9 = (bf16[1024,256]{1,0:T(8,128)(2,1)}, bf16[1024,256]{1,0:T(8,128)(2,1)S(1)}, u32[]{:S(2)}, u32[]{:S(2)}) collective-permute-start(bf16[1024,256]{1,0:T(8,128)(2,1)} %refs_6_.1), channel_id=1, source_target_pairs={{0,8},{8,0},{1,9},{9,1},{2,10},{10,2},{3,11},{11,3},{4,12},{12,4},... | collective-permute-start | bytes 1572872 | tf_op jit(solution)/shard_map/ppermute | solution.py:27
  18.0 7.7 %collective-permute-start.4 = (bf16[128,256]{1,0:T(8,128)(2,1)S(1)}, bf16[128,256]{1,0:T(8,128)(2,1)S(1)}, u32[]{:S(2)}, u32[]{:S(2)}) collective-permute-start(bf16[128,256]{1,0:T(8,128)(2,1)S(1)} %bitcast.21), channel_id=1, source_target_pairs={{0,1},{1,16},{16,17},{17,0},{2,3},{3,18},{18,19},{19,2},{4,5},{5,2... | collective-permute-start | bytes 196616 | tf_op jit(solution)/shard_map/ppermute | solution.py:34
  19.6 7.7 %collective-permute-start.5 = (bf16[128,256]{1,0:T(8,128)(2,1)S(1)}, bf16[128,256]{1,0:T(8,128)(2,1)S(1)}, u32[]{:S(2)}, u32[]{:S(2)}) collective-permute-start(bf16[128,256]{1,0:T(8,128)(2,1)S(1)} %bitcast.22), channel_id=1, source_target_pairs={{0,17},{1,0},{16,1},{17,16},{2,19},{3,2},{18,3},{19,18},{4,21},{5,... | collective-permute-start | bytes 196616 | tf_op jit(solution)/shard_map/ppermute | solution.py:34
  21.4 8.0 %collective-permute-start.6 = (bf16[128,256]{1,0:T(8,128)(2,1)S(1)}, bf16[128,256]{1,0:T(8,128)(2,1)S(1)}, u32[]{:S(2)}, u32[]{:S(2)}) collective-permute-start(bf16[128,256]{1,0:T(8,128)(2,1)S(1)} %bitcast.23), channel_id=1, source_target_pairs={{0,16},{1,17},{16,0},{17,1},{2,18},{3,19},{18,2},{19,3},{4,20},{5,... | collective-permute-start | bytes 196616 | tf_op jit(solution)/shard_map/ppermute | solution.py:34
  24.0 6.5 %collective-permute-start = (bf16[128,256]{1,0:T(8,128)(2,1)S(1)}, bf16[128,256]{1,0:T(8,128)(2,1)S(1)}, u32[]{:S(2)}, u32[]{:S(2)}) collective-permute-start(bf16[128,256]{1,0:T(8,128)(2,1)S(1)} %bitcast.17), channel_id=1, source_target_pairs={{0,2},{2,4},{4,6},{6,0},{1,3},{3,5},{5,7},{7,1},{8,10},{10,12},{12... | collective-permute-start | bytes 196616 | tf_op jit(solution)/shard_map/ppermute | solution.py:34
  25.7 6.5 %collective-permute-start.1 = (bf16[128,256]{1,0:T(8,128)(2,1)S(1)}, bf16[128,256]{1,0:T(8,128)(2,1)S(1)}, u32[]{:S(2)}, u32[]{:S(2)}) collective-permute-start(bf16[128,256]{1,0:T(8,128)(2,1)S(1)} %bitcast.18), channel_id=1, source_target_pairs={{0,6},{2,0},{4,2},{6,4},{1,7},{3,1},{5,3},{7,5},{8,14},{10,8},{12,... | collective-permute-start | bytes 196616 | tf_op jit(solution)/shard_map/ppermute | solution.py:34
  27.4 6.5 %collective-permute-start.2 = (bf16[128,256]{1,0:T(8,128)(2,1)S(1)}, bf16[128,256]{1,0:T(8,128)(2,1)S(1)}, u32[]{:S(2)}, u32[]{:S(2)}) collective-permute-start(bf16[128,256]{1,0:T(8,128)(2,1)S(1)} %bitcast.19), channel_id=1, source_target_pairs={{0,4},{2,6},{4,0},{6,2},{1,5},{3,7},{5,1},{7,3},{8,12},{10,14},{12... | collective-permute-start | bytes 196616 | tf_op jit(solution)/shard_map/ppermute | solution.py:34
  29.4 15.8 %collective-permute-start.13 = (bf16[512,256]{1,0:T(8,128)(2,1)S(1)}, bf16[512,256]{1,0:T(8,128)(2,1)S(1)}, u32[]{:S(2)}, u32[]{:S(2)}) collective-permute-start(bf16[512,256]{1,0:T(8,128)(2,1)S(1)} %pad_maximum_fusion.10.refs_2_), channel_id=1, source_target_pairs={{0,6},{2,0},{4,2},{6,4},{1,7},{3,1},{5,3},{7,5},{8,14},{10,8},{12,... | collective-permute-start | bytes 786440 | tf_op jit(solution)/shard_map/ppermute | solution.py:34
  30.5 22.1 %collective-permute-start.11 = (bf16[512,256]{1,0:T(8,128)(2,1)S(1)}, bf16[512,256]{1,0:T(8,128)(2,1)S(1)}, u32[]{:S(2)}, u32[]{:S(2)}) collective-permute-start(bf16[512,256]{1,0:T(8,128)(2,1)S(1)} %pad_maximum_fusion.10.refs_2_), channel_id=1, source_target_pairs={{0,4},{2,6},{4,0},{6,2},{1,5},{3,7},{5,1},{7,3},{8,12},{10,14},{12... | collective-permute-start | bytes 786440 | tf_op jit(solution)/shard_map/ppermute | solution.py:34
  33.9 12.1 %collective-permute-start.12 = (bf16[512,256]{1,0:T(8,128)(2,1)S(1)}, bf16[512,256]{1,0:T(8,128)(2,1)S(1)}, u32[]{:S(2)}, u32[]{:S(2)}) collective-permute-start(bf16[512,256]{1,0:T(8,128)(2,1)S(1)} %pad_maximum_fusion.9.refs_1_), channel_id=1, source_target_pairs={{0,17},{1,0},{16,1},{17,16},{2,19},{3,2},{18,3},{19,18},{4,21},{5,... | collective-permute-start | bytes 786440 | tf_op jit(solution)/shard_map/ppermute | solution.py:34
  35.1 17.6 %collective-permute-start.10 = (bf16[512,256]{1,0:T(8,128)(2,1)S(1)}, bf16[512,256]{1,0:T(8,128)(2,1)S(1)}, u32[]{:S(2)}, u32[]{:S(2)}) collective-permute-start(bf16[512,256]{1,0:T(8,128)(2,1)S(1)} %pad_maximum_fusion.9.refs_1_), channel_id=1, source_target_pairs={{0,16},{1,17},{16,0},{17,1},{2,18},{3,19},{18,2},{19,3},{4,20},{5,... | collective-permute-start | bytes 786440 | tf_op jit(solution)/shard_map/ppermute | solution.py:34
  36.6 25.5 %collective-permute-start.7 = (bf16[512,256]{1,0:T(8,128)(2,1)S(1)}, bf16[512,256]{1,0:T(8,128)(2,1)S(1)}, u32[]{:S(2)}, u32[]{:S(2)}) collective-permute-start(bf16[512,256]{1,0:T(8,128)(2,1)S(1)} %pad_maximum_fusion.10.refs_2_), channel_id=1, source_target_pairs={{0,2},{2,4},{4,6},{6,0},{1,3},{3,5},{5,7},{7,1},{8,10},{10,12},{12... | collective-permute-start | bytes 786440 | tf_op jit(solution)/shard_map/ppermute | solution.py:34
  37.2 1.0 copy-start
  45.2 16.9 %collective-permute-start.3 = (bf16[512,256]{1,0:T(8,128)(2,1)S(1)}, bf16[512,256]{1,0:T(8,128)(2,1)S(1)}, u32[]{:S(2)}, u32[]{:S(2)}) collective-permute-start(bf16[512,256]{1,0:T(8,128)(2,1)S(1)} %pad_maximum_fusion.9.refs_1_), channel_id=1, source_target_pairs={{0,1},{1,16},{16,17},{17,0},{2,3},{3,18},{18,19},{19,2},{4,5},{5,2... | collective-permute-start | bytes 786440 | tf_op jit(solution)/shard_map/ppermute | solution.py:34
  59.4 13.1 %collective-permute-start.24 = (f32[256,256]{1,0:T(8,128)}, f32[256,256]{1,0:T(8,128)S(1)}, u32[]{:S(2)}, u32[]{:S(2)}) collective-permute-start(f32[256,256]{1,0:T(8,128)} %get-tuple-element.52), channel_id=1, source_target_pairs={{0,6},{2,0},{4,2},{6,4},{1,7},{3,1},{5,3},{7,5},{8,14},{10,8},{12,... | collective-permute-start | bytes 786440 | tf_op jit(solution)/shard_map/ppermute | solution.py:34
  62.1 7.0 %copy-start.7 = (f32[256,256]{1,0:T(8,128)S(1)}, f32[256,256]{1,0:T(8,128)}, u32[]{:S(2)}) copy-start(f32[256,256]{1,0:T(8,128)} %get-tuple-element.49) | copy-start | bytes 786436
  62.1 8.6 %copy-start.6 = (f32[256,256]{1,0:T(8,128)S(1)}, f32[256,256]{1,0:T(8,128)}, u32[]{:S(2)}) copy-start(f32[256,256]{1,0:T(8,128)} %get-tuple-element.46) | copy-start | bytes 786436
  68.8 10.3 %copy-start.2 = (f32[512,256]{1,0:T(8,128)S(1)}, f32[512,256]{1,0:T(8,128)}, u32[]{:S(2)}) copy-start(f32[512,256]{1,0:T(8,128)} %get-tuple-element.53) | copy-start | bytes 1572868
  69.0 3.5 %collective-permute-start.16 = (f32[8,256]{1,0:T(8,128)S(1)}, f32[8,256]{1,0:T(8,128)S(1)}, u32[]{:S(2)}, u32[]{:S(2)}) collective-permute-start(f32[8,256]{1,0:T(8,128)S(1)} %scatter-add.4), channel_id=1, source_target_pairs={{0,8},{8,0},{1,9},{9,1},{2,10},{10,2},{3,11},{11,3},{4,12},{12,4},... | collective-permute-start | bytes 24584 | tf_op jit(solution)/shard_map/ppermute | solution.py:27
  69.1 10.1 %collective-permute-start.26 = (f32[256,256]{1,0:T(8,128)}, f32[256,256]{1,0:T(8,128)S(1)}, u32[]{:S(2)}, u32[]{:S(2)}) collective-permute-start(f32[256,256]{1,0:T(8,128)} %get-tuple-element.54), channel_id=1, source_target_pairs={{0,2},{2,4},{4,6},{6,0},{1,3},{3,5},{5,7},{7,1},{8,10},{10,12},{12... | collective-permute-start | bytes 786440 | tf_op jit(solution)/shard_map/ppermute | solution.py:34
  69.2 10.2 %collective-permute-start.18 = (f32[256,256]{1,0:T(8,128)S(1)}, f32[256,256]{1,0:T(8,128)S(1)}, u32[]{:S(2)}, u32[]{:S(2)}) collective-permute-start(f32[256,256]{1,0:T(8,128)S(1)} %copy-done.7), channel_id=1, source_target_pairs={{0,1},{1,16},{16,17},{17,0},{2,3},{3,18},{18,19},{19,2},{4,5},{5,2... | collective-permute-start | bytes 786440 | tf_op jit(solution)/shard_map/ppermute | solution.py:34
  70.7 8.7 %collective-permute-start.15 = (f32[256,256]{1,0:T(8,128)S(1)}, f32[256,256]{1,0:T(8,128)S(1)}, u32[]{:S(2)}, u32[]{:S(2)}) collective-permute-start(f32[256,256]{1,0:T(8,128)S(1)} %copy-done.6), channel_id=1, source_target_pairs={{0,17},{1,0},{16,1},{17,16},{2,19},{3,2},{18,3},{19,18},{4,21},{5,... | collective-permute-start | bytes 786440 | tf_op jit(solution)/shard_map/ppermute | solution.py:34
  72.5 6.9 %copy-start.1 = (f32[512,256]{1,0:T(8,128)S(1)}, f32[512,256]{1,0:T(8,128)}, u32[]{:S(2)}) copy-start(f32[512,256]{1,0:T(8,128)} %get-tuple-element.48) | copy-start | bytes 1572868
  73.7 5.8 %copy-start.3 = (f32[512,256]{1,0:T(8,128)S(1)}, f32[512,256]{1,0:T(8,128)}, u32[]{:S(2)}) copy-start(f32[512,256]{1,0:T(8,128)} %get-tuple-element.45) | copy-start | bytes 1572868
  73.7 14.1 %collective-permute-start.25 = (f32[512,256]{1,0:T(8,128)S(1)}, f32[512,256]{1,0:T(8,128)S(1)}, u32[]{:S(2)}, u32[]{:S(2)}) collective-permute-start(f32[512,256]{1,0:T(8,128)S(1)} %pad_maximum_fusion.2), channel_id=1, source_target_pairs={{0,6},{2,0},{4,2},{6,4},{1,7},{3,1},{5,3},{7,5},{8,14},{10,8},{12,... | collective-permute-start | bytes 1572872 | tf_op jit(solution)/shard_map/ppermute | solution.py:34
  79.3 14.7 %collective-permute-start.27 = (f32[512,256]{1,0:T(8,128)S(1)}, f32[512,256]{1,0:T(8,128)S(1)}, u32[]{:S(2)}, u32[]{:S(2)}) collective-permute-start(f32[512,256]{1,0:T(8,128)S(1)} %pad_maximum_fusion.3), channel_id=1, source_target_pairs={{0,2},{2,4},{4,6},{6,0},{1,3},{3,5},{5,7},{7,1},{8,10},{10,12},{12... | collective-permute-start | bytes 1572872 | tf_op jit(solution)/shard_map/ppermute | solution.py:34
  79.5 14.4 %copy-start.5 = (f32[512,256]{1,0:T(8,128)S(1)}, f32[512,256]{1,0:T(8,128)}, u32[]{:S(2)}) copy-start(f32[512,256]{1,0:T(8,128)} %get-tuple-element.50) | copy-start | bytes 1572868
  79.6 17.3 %collective-permute-start.17 = (f32[520,256]{1,0:T(8,128)S(1)}, f32[520,256]{1,0:T(8,128)S(1)}, u32[]{:S(2)}, u32[]{:S(2)}) collective-permute-start(f32[520,256]{1,0:T(8,128)S(1)} %get-tuple-element.84), channel_id=1, source_target_pairs={{0,17},{1,0},{16,1},{17,16},{2,19},{3,2},{18,3},{19,18},{4,21},{5,... | collective-permute-start | bytes 1597448 | tf_op jit(solution)/shard_map/ppermute | solution.py:34
  82.5 14.7 %collective-permute-start.19 = (f32[520,256]{1,0:T(8,128)S(1)}, f32[520,256]{1,0:T(8,128)S(1)}, u32[]{:S(2)}, u32[]{:S(2)}) collective-permute-start(f32[520,256]{1,0:T(8,128)S(1)} %get-tuple-element.85), channel_id=1, source_target_pairs={{0,1},{1,16},{16,17},{17,0},{2,3},{3,18},{18,19},{19,2},{4,5},{5,2... | collective-permute-start | bytes 1597448 | tf_op jit(solution)/shard_map/ppermute | solution.py:34
  82.5 16.8 %copy-start.4 = (f32[512,256]{1,0:T(8,128)S(1)}, f32[512,256]{1,0:T(8,128)}, u32[]{:S(2)}) copy-start(f32[512,256]{1,0:T(8,128)} %get-tuple-element.44) | copy-start | bytes 1572868
  83.6 34.1 %collective-permute-start.14 = (f32[256,1024]{1,0:T(8,128)}, f32[256,1024]{1,0:T(8,128)}, u32[]{:S(2)}, u32[]{:S(2)}) collective-permute-start(f32[256,1024]{1,0:T(8,128)} %slice.110), channel_id=1, source_target_pairs={{0,8},{8,0},{1,9},{9,1},{2,10},{10,2},{3,11},{11,3},{4,12},{12,4},... | collective-permute-start | bytes 3145736 | tf_op jit(solution)/shard_map/ppermute | solution.py:27
  87.8 11.6 %collective-permute-start.20 = (f32[8,256]{1,0:T(8,128)S(1)}, f32[8,256]{1,0:T(8,128)S(1)}, u32[]{:S(2)}, u32[]{:S(2)}) collective-permute-start(f32[8,256]{1,0:T(8,128)S(1)} %add.71), channel_id=1, source_target_pairs={{0,16},{1,17},{16,0},{17,1},{2,18},{3,19},{18,2},{19,3},{4,20},{5,... | collective-permute-start | bytes 24584 | tf_op jit(solution)/shard_map/ppermute | solution.py:34
  94.1 9.3 %collective-permute-start.28 = (f32[128,256]{1,0:T(8,128)S(1)}, f32[128,256]{1,0:T(8,128)S(1)}, u32[]{:S(2)}, u32[]{:S(2)}) collective-permute-start(f32[128,256]{1,0:T(8,128)S(1)} %get-tuple-element.63), channel_id=1, source_target_pairs={{0,17},{1,0},{16,1},{17,16},{2,19},{3,2},{18,3},{19,18},{4,21},{5,... | collective-permute-start | bytes 393224 | tf_op jit(solution)/shard_map/ppermute | solution.py:34
  97.0 7.8 %collective-permute-start.29 = (f32[128,256]{1,0:T(8,128)S(1)}, f32[128,256]{1,0:T(8,128)S(1)}, u32[]{:S(2)}, u32[]{:S(2)}) collective-permute-start(f32[128,256]{1,0:T(8,128)S(1)} %get-tuple-element.65), channel_id=1, source_target_pairs={{0,1},{1,16},{16,17},{17,0},{2,3},{3,18},{18,19},{19,2},{4,5},{5,2... | collective-permute-start | bytes 393224 | tf_op jit(solution)/shard_map/ppermute | solution.py:34
  97.2 7.8 %collective-permute-start.30 = (f32[128,256]{1,0:T(8,128)S(1)}, f32[128,256]{1,0:T(8,128)S(1)}, u32[]{:S(2)}, u32[]{:S(2)}) collective-permute-start(f32[128,256]{1,0:T(8,128)S(1)} %get-tuple-element.64), channel_id=1, source_target_pairs={{0,16},{1,17},{16,0},{17,1},{2,18},{3,19},{18,2},{19,3},{4,20},{5,... | collective-permute-start | bytes 393224 | tf_op jit(solution)/shard_map/ppermute | solution.py:34
  99.5 7.1 %collective-permute-start.21 = (f32[136,256]{1,0:T(8,128)S(1)}, f32[136,256]{1,0:T(8,128)S(1)}, u32[]{:S(2)}, u32[]{:S(2)}) collective-permute-start(f32[136,256]{1,0:T(8,128)S(1)} %get-tuple-element.81), channel_id=1, source_target_pairs={{0,6},{2,0},{4,2},{6,4},{1,7},{3,1},{5,3},{7,5},{8,14},{10,8},{12,... | collective-permute-start | bytes 417800 | tf_op jit(solution)/shard_map/ppermute | solution.py:34
  103.4 8.4 %collective-permute-start.22 = (f32[136,256]{1,0:T(8,128)S(1)}, f32[136,256]{1,0:T(8,128)S(1)}, u32[]{:S(2)}, u32[]{:S(2)}) collective-permute-start(f32[136,256]{1,0:T(8,128)S(1)} %get-tuple-element.82), channel_id=1, source_target_pairs={{0,2},{2,4},{4,6},{6,0},{1,3},{3,5},{5,7},{7,1},{8,10},{10,12},{12... | collective-permute-start | bytes 417800 | tf_op jit(solution)/shard_map/ppermute | solution.py:34
  104.8 7.0 %collective-permute-start.23 = (f32[136,256]{1,0:T(8,128)S(1)}, f32[136,256]{1,0:T(8,128)S(1)}, u32[]{:S(2)}, u32[]{:S(2)}) collective-permute-start(f32[136,256]{1,0:T(8,128)S(1)} %get-tuple-element.83), channel_id=1, source_target_pairs={{0,4},{2,6},{4,0},{6,2},{1,5},{3,7},{5,1},{7,3},{8,12},{10,14},{12... | collective-permute-start | bytes 417800 | tf_op jit(solution)/shard_map/ppermute | solution.py:34
  112.7 14.7 %all-to-all-start.1 = ((f32[8,40,256]{2,1,0:T(8,128)}), f32[8,40,256]{2,1,0:T(8,128)S(1)}, u32[]{:S(2)}, u32[]{:S(2)}) async-start(f32[8,40,256]{2,1,0:T(8,128)} %pad_maximum_fusion.4), calls=%async_computation.1 | async-start | bytes 655360 | tf_op jit(solution)/shard_map/all_to_all | solution.py:213
where the time goes:
time: 131 us; the launch traced here: 130 us
  starting transfers between devices  54.6 us (42%)
  waiting for transfers between devices  32.9 us (25%)
  Pallas kernels  27.1 us (21%)
  other arithmetic  8.46 us (6%)
  local copies, waits for them, and re-layouts  4.71 us (4%)
  between operations  2.79 us (2%)
    ppermute x27, starting transfers between devices, moved(): lax.ppermute(array, axes, [(i, (i + distance) % peers) for i in range(pee...  40.4 us
    pallas_call x4, Pallas kernels, fused(): pl.pallas_call(functools.partial(kernel, sizes, side, split), in_specs=[p...  27.1 us
    ppermute x27, waiting for transfers between devices, moved(): lax.ppermute(array, axes, [(i, (i + distance) % peers) for i in range(pee...  20.9 us
    all_to_all x1, starting transfers between devices, on_device(): lax.all_to_all(jnp.broadcast_to(documents[None], (n_z, piece, width)), 'z...  8.57 us
    all_to_all x1, waiting for transfers between devices, on_device(): part = lax.all_to_all(part, 'z', 0, 0, tiled=True).sum(0)  7.33 us
    all_to_all x1, starting transfers between devices, on_device(): part = lax.all_to_all(part, 'z', 0, 0, tiled=True).sum(0)  4.97 us
    all_to_all x1, waiting for transfers between devices, on_device(): lax.all_to_all(jnp.broadcast_to(documents[None], (n_z, piece, width)), 'z...  4.62 us
  transfers between devices with their start and end apart: 33, of which 10 were waited for; matrix products, arithmetic and copies ran while one was open for 7% of the time, Pallas kernels for 21%

commit v1 on v0

--- a/solution.py
+++ b/solution.py
@@ -36,9 +36,10 @@
 
 def kernel(sizes, side, split, *refs):
     n_x, n_y, n_z = sizes
-    place_ref, xd_ref, yd_ref, off_ref, w_ref, pos_ref, *refs = refs
+    first, last = side == SIDES_IN_TURN[0], side == SIDES_IN_TURN[-1]
+    place_ref, xd_ref, yd_ref, off_ref, w_ref, pos_ref, ends_ref, *refs = refs
     nq = off_ref.shape[1]
-    if side == SIDES_IN_TURN[0]:
+    if first:
         own_ref, other_ref, *refs = refs
     else:
         q_ref, qt_ref, gq_in, found_in, *refs = refs
@@ -47,16 +48,18 @@
     outs = nd // split
     gd_refs, refs = refs[:outs], refs[outs:]
     gq_ref, found_ref, *refs = refs
-    if side == SIDES_IN_TURN[0]:
+    if first:
         q_ref, qt_ref, *refs = refs
     dt_ref, id_ref, c_ref, gd_ref, sems = refs
 
-    if side == SIDES_IN_TURN[0]:
-        for i, ref in enumerate((own_ref, other_ref)):
-            part = slice(i * (nq // 2), (i + 1) * (nq // 2))
-            q_ref[part, :] = ref[...]
-            qt_ref[:, part] = ref[...].T
-    gd_ref[...] = jnp.zeros(gd_ref.shape, F32)
+    if first:
+        own = pltpu.make_async_copy(own_ref, q_ref.at[: nq // 2], sems.at[nd // SUB])
+        own.start()
+        q_ref[nq // 2 :, :] = other_ref[...]
+        qt_ref[:, nq // 2 :] = other_ref[...].T
+    if last:
+        top = lax.broadcasted_iota(jnp.int32, found_ref.shape, 0) == 0
+        found_ref[...] = jnp.where(top, ends_ref[...], 0.0)
     piece = half // (4 * n_z // 2)
     x, y, core = place_ref[0], place_ref[1], place_ref[2]
     row = lax.broadcasted_iota(jnp.int32, (piece, 128), 0)
@@ -70,6 +73,9 @@
         id_ref[block * piece : (block + 1) * piece, :] = row + base * piece
     for i, ref in enumerate((xd_ref, yd_ref)):
         dt_ref[:, i * half : (i + 1) * half] = ref[...].T
+    if first:
+        own.wait()
+        qt_ref[:, : nq // 2] = q_ref[: nq // 2, :].T
 
     def front(tile, slot):
         cols = pl.ds(pl.multiple_of(tile * QT, QT), QT)
@@ -79,59 +85,69 @@
         pos = pos_ref[:, cols]
         found = jnp.zeros((8, QT), F32)
         for r in range(0, nd, SUB):
-            rows = slice(r, r + SUB)
             docs = (xd_ref, yd_ref)[r // half][r % half : r % half + SUB, :]
             scores = jnp.dot(docs, q_t, preferred_element_type=F32)
             probs = jnp.exp2(scores * (0.0625 * LOG2E) - off)
-            hits = jnp.concatenate([id_ref[rows, :]] * (QT // 128), 1) == pos
-            c_ref[slot, rows, :] = (probs - jnp.where(hits, w, 0.0)).astype(BF16)
+            hits = jnp.concatenate([id_ref[r : r + SUB, :]] * (QT // 128), 1) == pos
+            c_ref[slot, r : r + SUB, :] = (probs - jnp.where(hits, w, 0.0)).astype(BF16)
             found = found + jnp.sum(jnp.where(hits, scores, 0.0).reshape(SUB // 8, 8, QT), 0)
-        found_ref[:, cols] = found if side == SIDES_IN_TURN[0] else found_in[:, cols] + found
-
-    def back(tile, slot):
+        if not first:
+            found = found_in[:, cols] + found
+        if last:
+            found_ref[...] -= 0.0625 * w * found
+        else:
+            found_ref[:, cols] = found
+
+    def back(tile, slot, opening=False, closing=False):
         cols = pl.ds(pl.multiple_of(tile * QT, QT), QT)
         q = q_ref[cols, :]
+        leave = []
         for r in range(0, nd, SUB):
-            gd_ref[r : r + SUB, :] += jnp.dot(c_ref[slot, r : r + SUB, :], q, preferred_element_type=F32)
+            rows = slice(r, r + SUB)
+            term = jnp.dot(c_ref[slot, rows, :], q, preferred_element_type=F32)
+            gd_ref[rows, :] = term if opening else gd_ref[rows, :] + term
+            if closing:
+                out = gd_refs[r // split].at[pl.ds(r % split, SUB)]
+                leave.append(pltpu.make_async_copy(gd_ref.at[rows], out, sems.at[r // SUB]))
+                leave[-1].start()
         term = jnp.dot(dt_ref[...], c_ref[slot], preferred_element_type=F32)
-        gq_ref[:, cols] = term if side == SIDES_IN_TURN[0] else gq_in[:, cols] + term
+        gq_ref[:, cols] = term if first else gq_in[:, cols] + term
+        for copy in leave:
+            copy.wait()
 
     tiles = nq // QT
     front(0, 0)
+    front(1, 1)
+    back(0, 0, opening=True)
 
     def pair(i, _):
-        front(2 * i + 1, 1)
-        back(2 * i, 0)
-        front((2 * i + 2) % tiles, 0)
-        back(2 * i + 1, 1)
+        tile = 2 * i + 1
+        front(tile + 1, 0)
+        back(tile, 1)
+        front(tile + 2, 1)
+        back(tile + 1, 0)
         return 0
 
-    lax.fori_loop(0, tiles // 2, pair, 0)
-    leave = [
-        pltpu.make_async_copy(gd_ref.at[pl.ds(i * split, split)], gd_refs[i], sems.at[i]) for i in range(outs)
-    ]
-    for copy in leave:
-        copy.start()
-    for copy in leave:
-        copy.wait()
-
-
-def fused(side, split, place, x_docs, y_docs, off, w, pos, extra, sizes):
+    lax.fori_loop(0, (tiles - 2) // 2, pair, 0)
+    back(tiles - 1, 1, closing=True)
+
+
+def fused(side, split, place, x_docs, y_docs, off, w, pos, ends, extra, sizes):
     nq = off.shape[1]
     width = x_docs.shape[1]
     nd = 2 * x_docs.shape[0]
     vmem = pl.BlockSpec(memory_space=pltpu.VMEM)
     hbm = pl.BlockSpec(memory_space=pltpu.HBM)
-    first = side == SIDES_IN_TURN[0]
-    operands = [place, x_docs, y_docs, off, w, pos, *extra]
+    first, last = side == SIDES_IN_TURN[0], side == SIDES_IN_TURN[-1]
+    operands = [place, x_docs, y_docs, off, w, pos, ends, *extra]
     outs = nd // split
     out_shape = [pltpu.HBM((split, width), F32)] * outs
-    out_shape += [jax.ShapeDtypeStruct((width, nq), F32), jax.ShapeDtypeStruct((8, nq), F32)]
+    out_shape += [jax.ShapeDtypeStruct((width, nq), F32), jax.ShapeDtypeStruct((8, QT if last else nq), F32)]
     if first:
         out_shape += [jax.ShapeDtypeStruct((nq, width), BF16), jax.ShapeDtypeStruct((width, nq), BF16)]
     return pl.pallas_call(
         functools.partial(kernel, sizes, side, split),
-        in_specs=[pl.BlockSpec(memory_space=pltpu.SMEM)] + [vmem] * (len(operands) - 1),
+        in_specs=[pl.BlockSpec(memory_space=pltpu.SMEM)] + [vmem] * 6 + [hbm if first else vmem] + [vmem] * (len(operands) - 8),
         out_specs=[hbm] * outs + [vmem] * (len(out_shape) - outs),
         out_shape=out_shape,
         scratch_shapes=[
@@ -139,9 +155,9 @@
             pltpu.VMEM((nd, 128), jnp.int32),
             pltpu.VMEM((2, nd, QT), BF16),
             pltpu.VMEM((nd, width), F32),
-            pltpu.SemaphoreType.DMA((outs,)),
+            pltpu.SemaphoreType.DMA((nd // SUB + 1,)),
         ],
-        input_output_aliases={} if first else {8: outs},
+        input_output_aliases={} if first else {9: outs},
         compiler_params=pltpu.CompilerParams(vmem_limit_bytes=VMEM_LIMIT),
         cost_estimate=pl.CostEstimate(flops=6 * nq * nd * width, bytes_accessed=8 << 20, transcendentals=nq * nd),
         name="fused",
@@ -175,20 +191,18 @@
 
     half = x_docs[0].shape[0]
     terms = {}
-    extra = (queries, other_queries)
+    ends = (weights * log_norms).reshape(-1, QT).sum(0)[None]
+    extra = (pltpu.with_memory_space_constraint(queries, pltpu.HBM), other_queries)
     for side in SIDES_IN_TURN:
         split = half // 2 if side == 2 else half
         outs = 2 * half // split
-        got = fused(side, split, place, x_docs[side], y_docs[side], off, w, pos, extra, (n_x, n_y, n_z))
+        got = fused(side, split, place, x_docs[side], y_docs[side], off, w, pos, ends, extra, (n_x, n_y, n_z))
         terms[side] = got[:outs]
         grad_q, found = got[outs : outs + 2]
         layouts = got[outs + 2 :] or layouts
         extra = (*layouts, grad_q, found)
 
-    ends = (weights * log_norms).reshape(-1, width).sum(0)
-    lost = -0.0625 * (w * found).reshape(8, -1, width).sum(1)
-    lost = lost.at[0].add(ends)
-    lost = lost + other_core(lost)
+    lost = found + other_core(found)
 
     def ring(own_term, ahead, behind, far_a, far_b, axes):
         n = half // 2

time: 131 us -> 132 us (level); the launches traced: 130 us -> 129 us
  starting transfers between devices: 54.6 us -> 56.9 us
    ppermute x27, starting transfers between devices: 40.4 us -> 42.7 us  [moved(): lax.ppermute(array, axes, [(i, (i + distance) % peers) for i in range(pee...]
  transfers between devices with their start and end apart: 33 -> 33, of which waited for: 10 -> 12; matrix products, arithmetic and copies ran while one was open for 7% -> 6% of each run, Pallas kernels for 21% -> 20%
where the time goes in v1:
time: 132 us; the launch traced here: 129 us
  starting transfers between devices  56.9 us (43%)
  waiting for transfers between devices  32.7 us (25%)
  Pallas kernels  25.8 us (20%)
  other arithmetic  7.31 us (6%)
  local copies, waits for them, and re-layouts  3.59 us (3%)
  between operations  2.8 us (2%)
    ppermute x27, starting transfers between devices, moved(): lax.ppermute(array, axes, [(i, (i + distance) % peers) for i in range(pee...  42.7 us
    pallas_call x4, Pallas kernels, fused(): pl.pallas_call(functools.partial(kernel, sizes, side, split), in_specs=[p...  25.8 us
    ppermute x27, waiting for transfers between devices, moved(): lax.ppermute(array, axes, [(i, (i + distance) % peers) for i in range(pee...  20.9 us
    all_to_all x1, starting transfers between devices, on_device(): lax.all_to_all(jnp.broadcast_to(documents[None], (n_z, piece, width)), 'z...  8.57 us
    all_to_all x1, waiting for transfers between devices, on_device(): part = lax.all_to_all(part, 'z', 0, 0, tiled=True).sum(0)  7.2 us
    all_to_all x1, starting transfers between devices, on_device(): part = lax.all_to_all(part, 'z', 0, 0, tiled=True).sum(0)  4.89 us
    all_to_all x1, waiting for transfers between devices, on_device(): lax.all_to_all(jnp.broadcast_to(documents[None], (n_z, piece, width)), 'z...  4.62 us
  transfers between devices with their start and end apart: 33, of which 12 were waited for; matrix products, arithmetic and copies ran while one was open for 6% of the time, Pallas kernels for 20%

profile of v1, /device:TPU:32, one launch (start us, length us, event | category | flops | bytes accessed | tf_op | source)
XLA Modules:
  0.0 129.1 jit_solution(8906619261103622438)
XLA Ops:
  0.6 1.4 %broadcast_in_dim.6 = bf16[8,32,256]{2,1,0:T(8,128)(2,1)} broadcast(bf16[32,256]{1,0:T(8,128)(2,1)} %param.6), dimensions={1,2} | broadcast | bytes 147456 | tf_op jit(solution)/shard_map/broadcast_in_dim | solution.py:185
  2.0 8.6 %all-to-all-start = ((bf16[8,32,256]{2,1,0:T(8,128)(2,1)}), bf16[8,32,256]{2,1,0:T(8,128)(2,1)S(1)}, u32[]{:S(2)}, u32[]{:S(2)}) async-start(bf16[8,32,256]{2,1,0:T(8,128)(2,1)} %broadcast_in_dim.6), calls=%async_computation | async-start | bytes 262144 | tf_op jit(solution)/shard_map/all_to_all | solution.py:185
  10.6 0.7 convert_element_type.15
  11.3 0.7 pad_maximum_fusion.12
  12.6 0.7 mul.24
  13.4 4.6 %all-to-all-done = bf16[8,32,256]{2,1,0:T(8,128)(2,1)S(1)} async-done(((bf16[8,32,256]{2,1,0:T(8,128)(2,1)}), bf16[8,32,256]{2,1,0:T(8,128)(2,1)S(1)}, u32[]{:S(2)}, u32[]{:S(2)}) %all-to-all-start) | async-done | bytes 131104 | tf_op jit(solution)/shard_map/all_to_all | solution.py:185
  18.0 3.1 %collective-permute-start.6 = (bf16[128,256]{1,0:T(8,128)(2,1)S(1)}, bf16[128,256]{1,0:T(8,128)(2,1)S(1)}, u32[]{:S(2)}, u32[]{:S(2)}) collective-permute-start(bf16[128,256]{1,0:T(8,128)(2,1)S(1)} %bitcast.21), channel_id=1, source_target_pairs={{0,16},{1,17},{16,0},{17,1},{2,18},{3,19},{18,2},{19,3},{4,20},{5,... | collective-permute-start | bytes 196616 | tf_op jit(solution)/shard_map/ppermute | solution.py:34
  21.2 1.1 collective-permute-start.5
  22.3 0.9 collective-permute-start.4
  23.2 0.9 fusion.8
  24.0 3.3 %collective-permute-start.2 = (bf16[128,256]{1,0:T(8,128)(2,1)S(1)}, bf16[128,256]{1,0:T(8,128)(2,1)S(1)}, u32[]{:S(2)}, u32[]{:S(2)}) collective-permute-start(bf16[128,256]{1,0:T(8,128)(2,1)S(1)} %bitcast.17), channel_id=1, source_target_pairs={{0,4},{2,6},{4,0},{6,2},{1,5},{3,7},{5,1},{7,3},{8,12},{10,14},{12... | collective-permute-start | bytes 196616 | tf_op jit(solution)/shard_map/ppermute | solution.py:34
  27.3 1.1 collective-permute-start.1
  28.4 1.0 collective-permute-start
  29.4 2.3 %collective-permute-start.13 = (bf16[512,256]{1,0:T(8,128)(2,1)S(1)}, bf16[512,256]{1,0:T(8,128)(2,1)S(1)}, u32[]{:S(2)}, u32[]{:S(2)}) collective-permute-start(bf16[512,256]{1,0:T(8,128)(2,1)S(1)} %pad_maximum_fusion.10.refs_2_), channel_id=1, source_target_pairs={{0,6},{2,0},{4,2},{6,4},{1,7},{3,1},{5,3},{7,5},{8,14},{10,8},{12,... | collective-permute-start | bytes 786440 | tf_op jit(solution)/shard_map/ppermute | solution.py:34
  31.7 1.4 %collective-permute-start.11 = (bf16[512,256]{1,0:T(8,128)(2,1)S(1)}, bf16[512,256]{1,0:T(8,128)(2,1)S(1)}, u32[]{:S(2)}, u32[]{:S(2)}) collective-permute-start(bf16[512,256]{1,0:T(8,128)(2,1)S(1)} %pad_maximum_fusion.10.refs_2_), channel_id=1, source_target_pairs={{0,4},{2,6},{4,0},{6,2},{1,5},{3,7},{5,1},{7,3},{8,12},{10,14},{12... | collective-permute-start | bytes 786440 | tf_op jit(solution)/shard_map/ppermute | solution.py:34
  33.1 1.4 %collective-permute-start.7 = (bf16[512,256]{1,0:T(8,128)(2,1)S(1)}, bf16[512,256]{1,0:T(8,128)(2,1)S(1)}, u32[]{:S(2)}, u32[]{:S(2)}) collective-permute-start(bf16[512,256]{1,0:T(8,128)(2,1)S(1)} %pad_maximum_fusion.10.refs_2_), channel_id=1, source_target_pairs={{0,2},{2,4},{4,6},{6,0},{1,3},{3,5},{5,7},{7,1},{8,10},{10,12},{12... | collective-permute-start | bytes 786440 | tf_op jit(solution)/shard_map/ppermute | solution.py:34
  34.5 2.2 %collective-permute-done = bf16[128,256]{1,0:T(8,128)(2,1)S(1)} collective-permute-done((bf16[128,256]{1,0:T(8,128)(2,1)S(1)}, bf16[128,256]{1,0:T(8,128)(2,1)S(1)}, u32[]{:S(2)}, u32[]{:S(2)}) %collective-permute-start) | collective-permute-done | bytes 65568 | tf_op jit(solution)/shard_map/ppermute | solution.py:34
  36.7 2.4 %collective-permute-start.12 = (bf16[512,256]{1,0:T(8,128)(2,1)S(1)}, bf16[512,256]{1,0:T(8,128)(2,1)S(1)}, u32[]{:S(2)}, u32[]{:S(2)}) collective-permute-start(bf16[512,256]{1,0:T(8,128)(2,1)S(1)} %pad_maximum_fusion.9.refs_1_), channel_id=1, source_target_pairs={{0,17},{1,0},{16,1},{17,16},{2,19},{3,2},{18,3},{19,18},{4,21},{5,... | collective-permute-start | bytes 786440 | tf_op jit(solution)/shard_map/ppermute | solution.py:34
  39.4 7.2 %fused.4 = (f32[512,256]{1,0:T(8,128)}, f32[512,256]{1,0:T(8,128)}, f32[256,2048]{1,0:T(8,128)S(1)}, f32[8,2048]{1,0:T(8,128)S(1)}, bf16[2048,256]{1,0:T(8,128)(2,1)S(1)}, /*index=5*/bf16[256,2048]{1,0:T(8,128)(2,1)S(1)}) custom-call(s32[3]{0:T(128)S(1)} %pad_add_fusion.refs_0_, bf16[512,256]{1,0:T(8,128)(2,1)S(1)} %pad_maximum_fusion.9.refs_1_, ...), custom_call_target="tpu_custom_call" | custom-call | flops 3221225472 | bytes 8388608 | tf_op jit(solution)/shard_map/fused/pallas_call | solution.py:148
  46.6 1.1 collective-permute-start.3
  47.8 6.1 %fused.5 = (f32[512,256]{1,0:T(8,128)}, f32[512,256]{1,0:T(8,128)}, f32[256,2048]{1,0:T(8,128)S(1)}, f32[8,2048]{1,0:T(8,128)S(1)}) custom-call(s32[3]{0:T(128)S(1)} %pad_add_fusion.refs_0_, bf16[512,256]{1,0:T(8,128)(2,1)S(1)} %collective-permute-done.12.refs_1_, ...), custom_call_target="tpu_custom_call", output_to_operand_aliasing={{2}: (9, {})} | custom-call | flops 3221225472 | bytes 8388608 | tf_op jit(solution)/shard_map/fused/pallas_call | solution.py:148
  53.9 6.2 %fused.6 = (f32[256,256]{1,0:T(8,128)}, f32[256,256]{1,0:T(8,128)}, f32[256,256]{1,0:T(8,128)}, f32[256,256]{1,0:T(8,128)}, f32[256,2048]{1,0:T(8,128)S(1)}, /*index=5*/f32[8,2048]{1,0:T(8,128)S(1)}) custom-call(s32[3]{0:T(128)S(1)} %pad_add_fusion.refs_0_, bf16[512,256]{1,0:T(8,128)(2,1)S(1)} %collective-permute-done.10.refs_1_, ...), custom_call_target="tpu_custom_call", output_to_operand_aliasing={{4}: (9, {})} | custom-call | flops 3221225472 | bytes 8388608 | tf_op jit(solution)/shard_map/fused/pallas_call | solution.py:148
  60.3 6.2 %fused.7 = (f32[512,256]{1,0:T(8,128)}, f32[512,256]{1,0:T(8,128)}, f32[256,2048]{1,0:T(8,128)S(1)}, f32[8,256]{1,0:T(8,128)S(1)}) custom-call(s32[3]{0:T(128)S(1)} %pad_add_fusion.refs_0_, bf16[512,256]{1,0:T(8,128)(2,1)S(1)} %collective-permute-done.3.refs_1_, ...), custom_call_target="tpu_custom_call", output_to_operand_aliasing={{2}: (9, {})} | custom-call | flops 3221225472 | bytes 8388608 | tf_op jit(solution)/shard_map/fused/pallas_call | solution.py:148
  66.6 2.5 %collective-permute-start.15 = (f32[256,256]{1,0:T(8,128)S(1)}, f32[256,256]{1,0:T(8,128)S(1)}, u32[]{:S(2)}, u32[]{:S(2)}) collective-permute-start(f32[256,256]{1,0:T(8,128)S(1)} %copy-done.7), channel_id=1, source_target_pairs={{0,17},{1,0},{16,1},{17,16},{2,19},{3,2},{18,3},{19,18},{4,21},{5,... | collective-permute-start | bytes 786440 | tf_op jit(solution)/shard_map/ppermute | solution.py:34
  69.1 3.2 %collective-permute-start.24 = (f32[256,256]{1,0:T(8,128)S(1)}, f32[256,256]{1,0:T(8,128)S(1)}, u32[]{:S(2)}, u32[]{:S(2)}) collective-permute-start(f32[256,256]{1,0:T(8,128)S(1)} %copy-done.8), channel_id=1, source_target_pairs={{0,6},{2,0},{4,2},{6,4},{1,7},{3,1},{5,3},{7,5},{8,14},{10,8},{12,... | collective-permute-start | bytes 786440 | tf_op jit(solution)/shard_map/ppermute | solution.py:34
  72.9 5.4 %collective-permute-done.24 = f32[256,256]{1,0:T(8,128)S(1)} collective-permute-done((f32[256,256]{1,0:T(8,128)S(1)}, f32[256,256]{1,0:T(8,128)S(1)}, u32[]{:S(2)}, u32[]{:S(2)}) %collective-permute-start.24) | collective-permute-done | bytes 262176 | tf_op jit(solution)/shard_map/ppermute | solution.py:34
  78.4 3.8 %collective-permute-start.25 = (f32[512,256]{1,0:T(8,128)S(1)}, f32[512,256]{1,0:T(8,128)S(1)}, u32[]{:S(2)}, u32[]{:S(2)}) collective-permute-start(f32[512,256]{1,0:T(8,128)S(1)} %pad_maximum_fusion.2), channel_id=1, source_target_pairs={{0,6},{2,0},{4,2},{6,4},{1,7},{3,1},{5,3},{7,5},{8,14},{10,8},{12,... | collective-permute-start | bytes 1572872 | tf_op jit(solution)/shard_map/ppermute | solution.py:34
  82.4 3.0 %collective-permute-start.17 = (f32[520,256]{1,0:T(8,128)S(1)}, f32[520,256]{1,0:T(8,128)S(1)}, u32[]{:S(2)}, u32[]{:S(2)}) collective-permute-start(f32[520,256]{1,0:T(8,128)S(1)} %get-tuple-element.72), channel_id=1, source_target_pairs={{0,17},{1,0},{16,1},{17,16},{2,19},{3,2},{18,3},{19,18},{4,21},{5,... | collective-permute-start | bytes 1597448 | tf_op jit(solution)/shard_map/ppermute | solution.py:34
  85.3 1.1 slice.93
  86.4 1.3 %collective-permute-done.27 = f32[512,256]{1,0:T(8,128)S(1)} collective-permute-done((f32[512,256]{1,0:T(8,128)S(1)}, f32[512,256]{1,0:T(8,128)S(1)}, u32[]{:S(2)}, u32[]{:S(2)}) %collective-permute-start.27) | collective-permute-done | bytes 524320 | tf_op jit(solution)/shard_map/ppermute | solution.py:34
  87.7 2.0 %collective-permute-start.20 = (f32[8,256]{1,0:T(8,128)S(1)}, f32[8,256]{1,0:T(8,128)S(1)}, u32[]{:S(2)}, u32[]{:S(2)}) collective-permute-start(f32[8,256]{1,0:T(8,128)S(1)} %add.63), channel_id=1, source_target_pairs={{0,16},{1,17},{16,0},{17,1},{2,18},{3,19},{18,2},{19,3},{4,20},{5,... | collective-permute-start | bytes 24584 | tf_op jit(solution)/shard_map/ppermute | solution.py:34
  89.8 3.0 %collective-permute-done.25 = f32[512,256]{1,0:T(8,128)S(1)} collective-permute-done((f32[512,256]{1,0:T(8,128)S(1)}, f32[512,256]{1,0:T(8,128)S(1)}, u32[]{:S(2)}, u32[]{:S(2)}) %collective-permute-start.25) | collective-permute-done | bytes 524320 | tf_op jit(solution)/shard_map/ppermute | solution.py:34
  92.9 2.7 %collective-permute-start.28 = (f32[128,256]{1,0:T(8,128)S(1)}, f32[128,256]{1,0:T(8,128)S(1)}, u32[]{:S(2)}, u32[]{:S(2)}) collective-permute-start(f32[128,256]{1,0:T(8,128)S(1)} %get-tuple-element.51), channel_id=1, source_target_pairs={{0,17},{1,0},{16,1},{17,16},{2,19},{3,2},{18,3},{19,18},{4,21},{5,... | collective-permute-start | bytes 393224 | tf_op jit(solution)/shard_map/ppermute | solution.py:34
  95.6 1.6 %collective-permute-done.17 = f32[520,256]{1,0:T(8,128)S(1)} collective-permute-done((f32[520,256]{1,0:T(8,128)S(1)}, f32[520,256]{1,0:T(8,128)S(1)}, u32[]{:S(2)}, u32[]{:S(2)}) %collective-permute-start.17) | collective-permute-done | bytes 532512 | tf_op jit(solution)/shard_map/ppermute | solution.py:34
  97.2 2.1 %collective-permute-start.30 = (f32[128,256]{1,0:T(8,128)S(1)}, f32[128,256]{1,0:T(8,128)S(1)}, u32[]{:S(2)}, u32[]{:S(2)}) collective-permute-start(f32[128,256]{1,0:T(8,128)S(1)} %get-tuple-element.52), channel_id=1, source_target_pairs={{0,16},{1,17},{16,0},{17,1},{2,18},{3,19},{18,2},{19,3},{4,20},{5,... | collective-permute-start | bytes 393224 | tf_op jit(solution)/shard_map/ppermute | solution.py:34
  99.3 1.4 %collective-permute-done.19 = f32[520,256]{1,0:T(8,128)S(1)} collective-permute-done((f32[520,256]{1,0:T(8,128)S(1)}, f32[520,256]{1,0:T(8,128)S(1)}, u32[]{:S(2)}, u32[]{:S(2)}) %collective-permute-start.19) | collective-permute-done | bytes 532512 | tf_op jit(solution)/shard_map/ppermute | solution.py:34
  100.7 1.0 collective-permute-start.29
  102.1 2.0 %collective-permute-start.22 = (f32[136,256]{1,0:T(8,128)S(1)}, f32[136,256]{1,0:T(8,128)S(1)}, u32[]{:S(2)}, u32[]{:S(2)}) collective-permute-start(f32[136,256]{1,0:T(8,128)S(1)} %get-tuple-element.70), channel_id=1, source_target_pairs={{0,2},{2,4},{4,6},{6,0},{1,3},{3,5},{5,7},{7,1},{8,10},{10,12},{12... | collective-permute-start | bytes 417800 | tf_op jit(solution)/shard_map/ppermute | solution.py:34
  104.7 2.2 %collective-permute-done.29 = f32[128,256]{1,0:T(8,128)S(1)} collective-permute-done((f32[128,256]{1,0:T(8,128)S(1)}, f32[128,256]{1,0:T(8,128)S(1)}, u32[]{:S(2)}, u32[]{:S(2)}) %collective-permute-start.29) | collective-permute-done | bytes 131104 | tf_op jit(solution)/shard_map/ppermute | solution.py:34
  107.1 1.3 %collective-permute-done.22 = f32[136,256]{1,0:T(8,128)S(1)} collective-permute-done((f32[136,256]{1,0:T(8,128)S(1)}, f32[136,256]{1,0:T(8,128)S(1)}, u32[]{:S(2)}, u32[]{:S(2)}) %collective-permute-start.22) | collective-permute-done | bytes 139296 | tf_op jit(solution)/shard_map/ppermute | solution.py:34
  108.4 2.2 %collective-permute-done.23 = f32[136,256]{1,0:T(8,128)S(1)} collective-permute-done((f32[136,256]{1,0:T(8,128)S(1)}, f32[136,256]{1,0:T(8,128)S(1)}, u32[]{:S(2)}, u32[]{:S(2)}) %collective-permute-start.23) | collective-permute-done | bytes 139296 | tf_op jit(solution)/shard_map/ppermute | solution.py:34
  110.7 0.8 pad_maximum_fusion.4
  111.5 4.9 %all-to-all-start.1 = ((f32[8,40,256]{2,1,0:T(8,128)}), f32[8,40,256]{2,1,0:T(8,128)S(1)}, u32[]{:S(2)}, u32[]{:S(2)}) async-start(f32[8,40,256]{2,1,0:T(8,128)} %pad_maximum_fusion.4), calls=%async_computation.1 | async-start | bytes 655360 | tf_op jit(solution)/shard_map/all_to_all | solution.py:227
  116.4 1.4 %fusion = bf16[1024,256]{0,1:T(8,128)(2,1)S(1)} fusion(f32[256,1024]{1,0:T(8,128)} %collective-permute-done.14, f32[256,2048]{1,0:T(8,128)S(1)} %get-tuple-element.31), kind=kLoop, calls=%fused_computation.3 | loop fusion | flops 786432 | bytes 2621440 | tf_op jit(solution)/shard_map/convert_element_type | solution.py:232
  117.8 1.0 copy.12
  118.8 7.2 %all-to-all-done.1 = f32[8,40,256]{2,1,0:T(8,128)S(1)} async-done(((f32[8,40,256]{2,1,0:T(8,128)}), f32[8,40,256]{2,1,0:T(8,128)S(1)}, u32[]{:S(2)}, u32[]{:S(2)}) %all-to-all-start.1) | async-done | bytes 327712 | tf_op jit(solution)/shard_map/all_to_all | solution.py:227
  126.1 0.6 slice_reduce_fusion
  126.7 0.6 fusion.6
  (78 shorter events, 3.4 us)
Async XLA Ops:
  2.0 16.0 %all-to-all-start = ((bf16[8,32,256]{2,1,0:T(8,128)(2,1)}), bf16[8,32,256]{2,1,0:T(8,128)(2,1)S(1)}, u32[]{:S(2)}, u32[]{:S(2)}) async-start(bf16[8,32,256]{2,1,0:T(8,128)(2,1)} %broadcast_in_dim.6), calls=%async_computation | async-start | bytes 262144 | tf_op jit(solution)/shard_map/all_to_all | solution.py:185
  12.0 11.2 %collective-permute-start.8 = (f32[3,1024]{1,0:T(4,128)S(1)}, f32[3,1024]{1,0:T(4,128)S(1)}, u32[]{:S(2)}, u32[]{:S(2)}) collective-permute-start(f32[3,1024]{1,0:T(4,128)S(1)} %pad_maximum_fusion.12), channel_id=1, source_target_pairs={{0,8},{8,0},{1,9},{9,1},{2,10},{10,2},{3,11},{11,3},{4,12},{12,4},... | collective-permute-start | bytes 36872 | tf_op jit(solution)/shard_map/ppermute | solution.py:27
  12.1 27.0 %collective-permute-start.9 = (bf16[1024,256]{1,0:T(8,128)(2,1)}, bf16[1024,256]{1,0:T(8,128)(2,1)S(1)}, u32[]{:S(2)}, u32[]{:S(2)}) collective-permute-start(bf16[1024,256]{1,0:T(8,128)(2,1)} %refs_7_.1), channel_id=1, source_target_pairs={{0,8},{8,0},{1,9},{9,1},{2,10},{10,2},{3,11},{11,3},{4,12},{12,4},... | collective-permute-start | bytes 1572872 | tf_op jit(solution)/shard_map/ppermute | solution.py:27
  18.0 9.3 %collective-permute-start.6 = (bf16[128,256]{1,0:T(8,128)(2,1)S(1)}, bf16[128,256]{1,0:T(8,128)(2,1)S(1)}, u32[]{:S(2)}, u32[]{:S(2)}) collective-permute-start(bf16[128,256]{1,0:T(8,128)(2,1)S(1)} %bitcast.21), channel_id=1, source_target_pairs={{0,16},{1,17},{16,0},{17,1},{2,18},{3,19},{18,2},{19,3},{4,20},{5,... | collective-permute-start | bytes 196616 | tf_op jit(solution)/shard_map/ppermute | solution.py:34
  21.2 7.2 %collective-permute-start.5 = (bf16[128,256]{1,0:T(8,128)(2,1)S(1)}, bf16[128,256]{1,0:T(8,128)(2,1)S(1)}, u32[]{:S(2)}, u32[]{:S(2)}) collective-permute-start(bf16[128,256]{1,0:T(8,128)(2,1)S(1)} %bitcast.22), channel_id=1, source_target_pairs={{0,17},{1,0},{16,1},{17,16},{2,19},{3,2},{18,3},{19,18},{4,21},{5,... | collective-permute-start | bytes 196616 | tf_op jit(solution)/shard_map/ppermute | solution.py:34
  22.3 7.1 %collective-permute-start.4 = (bf16[128,256]{1,0:T(8,128)(2,1)S(1)}, bf16[128,256]{1,0:T(8,128)(2,1)S(1)}, u32[]{:S(2)}, u32[]{:S(2)}) collective-permute-start(bf16[128,256]{1,0:T(8,128)(2,1)S(1)} %bitcast.23), channel_id=1, source_target_pairs={{0,1},{1,16},{16,17},{17,0},{2,3},{3,18},{18,19},{19,2},{4,5},{5,2... | collective-permute-start | bytes 196616 | tf_op jit(solution)/shard_map/ppermute | solution.py:34
  24.0 7.7 %collective-permute-start.2 = (bf16[128,256]{1,0:T(8,128)(2,1)S(1)}, bf16[128,256]{1,0:T(8,128)(2,1)S(1)}, u32[]{:S(2)}, u32[]{:S(2)}) collective-permute-start(bf16[128,256]{1,0:T(8,128)(2,1)S(1)} %bitcast.17), channel_id=1, source_target_pairs={{0,4},{2,6},{4,0},{6,2},{1,5},{3,7},{5,1},{7,3},{8,12},{10,14},{12... | collective-permute-start | bytes 196616 | tf_op jit(solution)/shard_map/ppermute | solution.py:34
  27.3 5.8 %collective-permute-start.1 = (bf16[128,256]{1,0:T(8,128)(2,1)S(1)}, bf16[128,256]{1,0:T(8,128)(2,1)S(1)}, u32[]{:S(2)}, u32[]{:S(2)}) collective-permute-start(bf16[128,256]{1,0:T(8,128)(2,1)S(1)} %bitcast.18), channel_id=1, source_target_pairs={{0,6},{2,0},{4,2},{6,4},{1,7},{3,1},{5,3},{7,5},{8,14},{10,8},{12,... | collective-permute-start | bytes 196616 | tf_op jit(solution)/shard_map/ppermute | solution.py:34
  28.4 8.3 %collective-permute-start = (bf16[128,256]{1,0:T(8,128)(2,1)S(1)}, bf16[128,256]{1,0:T(8,128)(2,1)S(1)}, u32[]{:S(2)}, u32[]{:S(2)}) collective-permute-start(bf16[128,256]{1,0:T(8,128)(2,1)S(1)} %bitcast.19), channel_id=1, source_target_pairs={{0,2},{2,4},{4,6},{6,0},{1,3},{3,5},{5,7},{7,1},{8,10},{10,12},{12... | collective-permute-start | bytes 196616 | tf_op jit(solution)/shard_map/ppermute | solution.py:34
  29.4 17.2 %collective-permute-start.13 = (bf16[512,256]{1,0:T(8,128)(2,1)S(1)}, bf16[512,256]{1,0:T(8,128)(2,1)S(1)}, u32[]{:S(2)}, u32[]{:S(2)}) collective-permute-start(bf16[512,256]{1,0:T(8,128)(2,1)S(1)} %pad_maximum_fusion.10.refs_2_), channel_id=1, source_target_pairs={{0,6},{2,0},{4,2},{6,4},{1,7},{3,1},{5,3},{7,5},{8,14},{10,8},{12,... | collective-permute-start | bytes 786440 | tf_op jit(solution)/shard_map/ppermute | solution.py:34
  31.7 22.2 %collective-permute-start.11 = (bf16[512,256]{1,0:T(8,128)(2,1)S(1)}, bf16[512,256]{1,0:T(8,128)(2,1)S(1)}, u32[]{:S(2)}, u32[]{:S(2)}) collective-permute-start(bf16[512,256]{1,0:T(8,128)(2,1)S(1)} %pad_maximum_fusion.10.refs_2_), channel_id=1, source_target_pairs={{0,4},{2,6},{4,0},{6,2},{1,5},{3,7},{5,1},{7,3},{8,12},{10,14},{12... | collective-permute-start | bytes 786440 | tf_op jit(solution)/shard_map/ppermute | solution.py:34
  33.1 27.1 %collective-permute-start.7 = (bf16[512,256]{1,0:T(8,128)(2,1)S(1)}, bf16[512,256]{1,0:T(8,128)(2,1)S(1)}, u32[]{:S(2)}, u32[]{:S(2)}) collective-permute-start(bf16[512,256]{1,0:T(8,128)(2,1)S(1)} %pad_maximum_fusion.10.refs_2_), channel_id=1, source_target_pairs={{0,2},{2,4},{4,6},{6,0},{1,3},{3,5},{5,7},{7,1},{8,10},{10,12},{12... | collective-permute-start | bytes 786440 | tf_op jit(solution)/shard_map/ppermute | solution.py:34
  36.7 11.1 %collective-permute-start.12 = (bf16[512,256]{1,0:T(8,128)(2,1)S(1)}, bf16[512,256]{1,0:T(8,128)(2,1)S(1)}, u32[]{:S(2)}, u32[]{:S(2)}) collective-permute-start(bf16[512,256]{1,0:T(8,128)(2,1)S(1)} %pad_maximum_fusion.9.refs_1_), channel_id=1, source_target_pairs={{0,17},{1,0},{16,1},{17,16},{2,19},{3,2},{18,3},{19,18},{4,21},{5,... | collective-permute-start | bytes 786440 | tf_op jit(solution)/shard_map/ppermute | solution.py:34
  39.1 14.8 %collective-permute-start.10 = (bf16[512,256]{1,0:T(8,128)(2,1)S(1)}, bf16[512,256]{1,0:T(8,128)(2,1)S(1)}, u32[]{:S(2)}, u32[]{:S(2)}) collective-permute-start(bf16[512,256]{1,0:T(8,128)(2,1)S(1)} %pad_maximum_fusion.9.refs_1_), channel_id=1, source_target_pairs={{0,16},{1,17},{16,0},{17,1},{2,18},{3,19},{18,2},{19,3},{4,20},{5,... | collective-permute-start | bytes 786440 | tf_op jit(solution)/shard_map/ppermute | solution.py:34
  46.6 13.6 %collective-permute-start.3 = (bf16[512,256]{1,0:T(8,128)(2,1)S(1)}, bf16[512,256]{1,0:T(8,128)(2,1)S(1)}, u32[]{:S(2)}, u32[]{:S(2)}) collective-permute-start(bf16[512,256]{1,0:T(8,128)(2,1)S(1)} %pad_maximum_fusion.9.refs_1_), channel_id=1, source_target_pairs={{0,1},{1,16},{16,17},{17,0},{2,3},{3,18},{18,19},{19,2},{4,5},{5,2... | collective-permute-start | bytes 786440 | tf_op jit(solution)/shard_map/ppermute | solution.py:34
  60.1 12.3 %collective-permute-start.26 = (f32[256,256]{1,0:T(8,128)}, f32[256,256]{1,0:T(8,128)S(1)}, u32[]{:S(2)}, u32[]{:S(2)}) collective-permute-start(f32[256,256]{1,0:T(8,128)} %get-tuple-element.42), channel_id=1, source_target_pairs={{0,2},{2,4},{4,6},{6,0},{1,3},{3,5},{5,7},{7,1},{8,10},{10,12},{12... | collective-permute-start | bytes 786440 | tf_op jit(solution)/shard_map/ppermute | solution.py:34
  60.2 6.4 %copy-start.7 = (f32[256,256]{1,0:T(8,128)S(1)}, f32[256,256]{1,0:T(8,128)}, u32[]{:S(2)}) copy-start(f32[256,256]{1,0:T(8,128)} %get-tuple-element.34) | copy-start | bytes 786436
  60.3 8.8 %copy-start.6 = (f32[256,256]{1,0:T(8,128)S(1)}, f32[256,256]{1,0:T(8,128)}, u32[]{:S(2)}) copy-start(f32[256,256]{1,0:T(8,128)} %get-tuple-element.37) | copy-start | bytes 786436
  60.3 8.9 %copy-start.8 = (f32[256,256]{1,0:T(8,128)S(1)}, f32[256,256]{1,0:T(8,128)}, u32[]{:S(2)}) copy-start(f32[256,256]{1,0:T(8,128)} %get-tuple-element.40) | copy-start | bytes 786436
  60.3 12.1 %copy-start.1 = (f32[512,256]{1,0:T(8,128)S(1)}, f32[512,256]{1,0:T(8,128)}, u32[]{:S(2)}) copy-start(f32[512,256]{1,0:T(8,128)} %get-tuple-element.41) | copy-start | bytes 1572868
  66.5 11.7 %copy-start.3 = (f32[512,256]{1,0:T(8,128)S(1)}, f32[512,256]{1,0:T(8,128)}, u32[]{:S(2)}) copy-start(f32[512,256]{1,0:T(8,128)} %get-tuple-element.39) | copy-start | bytes 1572868
  66.5 5.9 %collective-permute-start.16 = (f32[8,256]{1,0:T(8,128)S(1)}, f32[8,256]{1,0:T(8,128)S(1)}, u32[]{:S(2)}, u32[]{:S(2)}) collective-permute-start(f32[8,256]{1,0:T(8,128)S(1)} %get-tuple-element.35), channel_id=1, source_target_pairs={{0,8},{8,0},{1,9},{9,1},{2,10},{10,2},{3,11},{11,3},{4,12},{12,4},... | collective-permute-start | bytes 24584 | tf_op jit(solution)/shard_map/ppermute | solution.py:27
  66.6 15.5 %collective-permute-start.15 = (f32[256,256]{1,0:T(8,128)S(1)}, f32[256,256]{1,0:T(8,128)S(1)}, u32[]{:S(2)}, u32[]{:S(2)}) collective-permute-start(f32[256,256]{1,0:T(8,128)S(1)} %copy-done.7), channel_id=1, source_target_pairs={{0,17},{1,0},{16,1},{17,16},{2,19},{3,2},{18,3},{19,18},{4,21},{5,... | collective-permute-start | bytes 786440 | tf_op jit(solution)/shard_map/ppermute | solution.py:34
  69.1 13.1 %collective-permute-start.18 = (f32[256,256]{1,0:T(8,128)S(1)}, f32[256,256]{1,0:T(8,128)S(1)}, u32[]{:S(2)}, u32[]{:S(2)}) collective-permute-start(f32[256,256]{1,0:T(8,128)S(1)} %copy-done.6), channel_id=1, source_target_pairs={{0,1},{1,16},{16,17},{17,0},{2,3},{3,18},{18,19},{19,2},{4,5},{5,2... | collective-permute-start | bytes 786440 | tf_op jit(solution)/shard_map/ppermute | solution.py:34
  69.1 9.1 %collective-permute-start.24 = (f32[256,256]{1,0:T(8,128)S(1)}, f32[256,256]{1,0:T(8,128)S(1)}, u32[]{:S(2)}, u32[]{:S(2)}) collective-permute-start(f32[256,256]{1,0:T(8,128)S(1)} %copy-done.8), channel_id=1, source_target_pairs={{0,6},{2,0},{4,2},{6,4},{1,7},{3,1},{5,3},{7,5},{8,14},{10,8},{12,... | collective-permute-start | bytes 786440 | tf_op jit(solution)/shard_map/ppermute | solution.py:34
  72.4 9.7 %copy-start.2 = (f32[512,256]{1,0:T(8,128)S(1)}, f32[512,256]{1,0:T(8,128)}, u32[]{:S(2)}) copy-start(f32[512,256]{1,0:T(8,128)} %get-tuple-element.33) | copy-start | bytes 1572868
  72.5 9.7 %copy-start = (f32[512,256]{1,0:T(8,128)S(1)}, f32[512,256]{1,0:T(8,128)}, u32[]{:S(2)}) copy-start(f32[512,256]{1,0:T(8,128)} %get-tuple-element.36) | copy-start | bytes 1572868
  72.5 15.2 %collective-permute-start.27 = (f32[512,256]{1,0:T(8,128)S(1)}, f32[512,256]{1,0:T(8,128)S(1)}, u32[]{:S(2)}, u32[]{:S(2)}) collective-permute-start(f32[512,256]{1,0:T(8,128)S(1)} %pad_maximum_fusion.3), channel_id=1, source_target_pairs={{0,2},{2,4},{4,6},{6,0},{1,3},{3,5},{5,7},{7,1},{8,10},{10,12},{12... | collective-permute-start | bytes 1572872 | tf_op jit(solution)/shard_map/ppermute | solution.py:34
  78.4 14.4 %collective-permute-start.25 = (f32[512,256]{1,0:T(8,128)S(1)}, f32[512,256]{1,0:T(8,128)S(1)}, u32[]{:S(2)}, u32[]{:S(2)}) collective-permute-start(f32[512,256]{1,0:T(8,128)S(1)} %pad_maximum_fusion.2), channel_id=1, source_target_pairs={{0,6},{2,0},{4,2},{6,4},{1,7},{3,1},{5,3},{7,5},{8,14},{10,8},{12,... | collective-permute-start | bytes 1572872 | tf_op jit(solution)/shard_map/ppermute | solution.py:34
  82.3 10.5 %copy-start.5 = (f32[512,256]{1,0:T(8,128)S(1)}, f32[512,256]{1,0:T(8,128)}, u32[]{:S(2)}) copy-start(f32[512,256]{1,0:T(8,128)} %get-tuple-element.38) | copy-start | bytes 1572868
  82.4 14.8 %collective-permute-start.17 = (f32[520,256]{1,0:T(8,128)S(1)}, f32[520,256]{1,0:T(8,128)S(1)}, u32[]{:S(2)}, u32[]{:S(2)}) collective-permute-start(f32[520,256]{1,0:T(8,128)S(1)} %get-tuple-element.72), channel_id=1, source_target_pairs={{0,17},{1,0},{16,1},{17,16},{2,19},{3,2},{18,3},{19,18},{4,21},{5,... | collective-permute-start | bytes 1597448 | tf_op jit(solution)/shard_map/ppermute | solution.py:34
  85.3 15.3 %collective-permute-start.19 = (f32[520,256]{1,0:T(8,128)S(1)}, f32[520,256]{1,0:T(8,128)S(1)}, u32[]{:S(2)}, u32[]{:S(2)}) collective-permute-start(f32[520,256]{1,0:T(8,128)S(1)} %get-tuple-element.73), channel_id=1, source_target_pairs={{0,1},{1,16},{16,17},{17,0},{2,3},{3,18},{18,19},{19,2},{4,5},{5,2... | collective-permute-start | bytes 1597448 | tf_op jit(solution)/shard_map/ppermute | solution.py:34
  85.3 16.4 %copy-start.4 = (f32[512,256]{1,0:T(8,128)S(1)}, f32[512,256]{1,0:T(8,128)}, u32[]{:S(2)}) copy-start(f32[512,256]{1,0:T(8,128)} %get-tuple-element.32) | copy-start | bytes 1572868
  86.4 30.0 %collective-permute-start.14 = (f32[256,1024]{1,0:T(8,128)}, f32[256,1024]{1,0:T(8,128)}, u32[]{:S(2)}, u32[]{:S(2)}) collective-permute-start(f32[256,1024]{1,0:T(8,128)} %slice.93), channel_id=1, source_target_pairs={{0,8},{8,0},{1,9},{9,1},{2,10},{10,2},{3,11},{11,3},{4,12},{12,4},... | collective-permute-start | bytes 3145736 | tf_op jit(solution)/shard_map/ppermute | solution.py:27
  87.7 14.2 %collective-permute-start.20 = (f32[8,256]{1,0:T(8,128)S(1)}, f32[8,256]{1,0:T(8,128)S(1)}, u32[]{:S(2)}, u32[]{:S(2)}) collective-permute-start(f32[8,256]{1,0:T(8,128)S(1)} %add.63), channel_id=1, source_target_pairs={{0,16},{1,17},{16,0},{17,1},{2,18},{3,19},{18,2},{19,3},{4,20},{5,... | collective-permute-start | bytes 24584 | tf_op jit(solution)/shard_map/ppermute | solution.py:34
  92.9 9.1 %collective-permute-start.28 = (f32[128,256]{1,0:T(8,128)S(1)}, f32[128,256]{1,0:T(8,128)S(1)}, u32[]{:S(2)}, u32[]{:S(2)}) collective-permute-start(f32[128,256]{1,0:T(8,128)S(1)} %get-tuple-element.51), channel_id=1, source_target_pairs={{0,17},{1,0},{16,1},{17,16},{2,19},{3,2},{18,3},{19,18},{4,21},{5,... | collective-permute-start | bytes 393224 | tf_op jit(solution)/shard_map/ppermute | solution.py:34
  97.2 6.9 %collective-permute-start.30 = (f32[128,256]{1,0:T(8,128)S(1)}, f32[128,256]{1,0:T(8,128)S(1)}, u32[]{:S(2)}, u32[]{:S(2)}) collective-permute-start(f32[128,256]{1,0:T(8,128)S(1)} %get-tuple-element.52), channel_id=1, source_target_pairs={{0,16},{1,17},{16,0},{17,1},{2,18},{3,19},{18,2},{19,3},{4,20},{5,... | collective-permute-start | bytes 393224 | tf_op jit(solution)/shard_map/ppermute | solution.py:34
  100.7 6.2 %collective-permute-start.29 = (f32[128,256]{1,0:T(8,128)S(1)}, f32[128,256]{1,0:T(8,128)S(1)}, u32[]{:S(2)}, u32[]{:S(2)}) collective-permute-start(f32[128,256]{1,0:T(8,128)S(1)} %get-tuple-element.53), channel_id=1, source_target_pairs={{0,1},{1,16},{16,17},{17,0},{2,3},{3,18},{18,19},{19,2},{4,5},{5,2... | collective-permute-start | bytes 393224 | tf_op jit(solution)/shard_map/ppermute | solution.py:34
  102.0 5.1 %collective-permute-start.21 = (f32[136,256]{1,0:T(8,128)S(1)}, f32[136,256]{1,0:T(8,128)S(1)}, u32[]{:S(2)}, u32[]{:S(2)}) collective-permute-start(f32[136,256]{1,0:T(8,128)S(1)} %get-tuple-element.69), channel_id=1, source_target_pairs={{0,6},{2,0},{4,2},{6,4},{1,7},{3,1},{5,3},{7,5},{8,14},{10,8},{12,... | collective-permute-start | bytes 417800 | tf_op jit(solution)/shard_map/ppermute | solution.py:34
  102.1 6.3 %collective-permute-start.22 = (f32[136,256]{1,0:T(8,128)S(1)}, f32[136,256]{1,0:T(8,128)S(1)}, u32[]{:S(2)}, u32[]{:S(2)}) collective-permute-start(f32[136,256]{1,0:T(8,128)S(1)} %get-tuple-element.70), channel_id=1, source_target_pairs={{0,2},{2,4},{4,6},{6,0},{1,3},{3,5},{5,7},{7,1},{8,10},{10,12},{12... | collective-permute-start | bytes 417800 | tf_op jit(solution)/shard_map/ppermute | solution.py:34
  104.1 6.6 %collective-permute-start.23 = (f32[136,256]{1,0:T(8,128)S(1)}, f32[136,256]{1,0:T(8,128)S(1)}, u32[]{:S(2)}, u32[]{:S(2)}) collective-permute-start(f32[136,256]{1,0:T(8,128)S(1)} %get-tuple-element.71), channel_id=1, source_target_pairs={{0,4},{2,6},{4,0},{6,2},{1,5},{3,7},{5,1},{7,3},{8,12},{10,14},{12... | collective-permute-start | bytes 417800 | tf_op jit(solution)/shard_map/ppermute | solution.py:34
  111.5 14.5 %all-to-all-start.1 = ((f32[8,40,256]{2,1,0:T(8,128)}), f32[8,40,256]{2,1,0:T(8,128)S(1)}, u32[]{:S(2)}, u32[]{:S(2)}) async-start(f32[8,40,256]{2,1,0:T(8,128)} %pad_maximum_fusion.4), calls=%async_computation.1 | async-start | bytes 655360 | tf_op jit(solution)/shard_map/all_to_all | solution.py:227

commit v2 on v1

--- a/solution.py
+++ b/solution.py
@@ -34,29 +34,56 @@
     return lax.ppermute(array, axes, [(i, (i + distance) % peers) for i in range(peers)])
 
 
+def layout_kernel(own_ref, other_ref, rows_ref, other_rows_ref, q_ref, qt_ref, off_ref, w_ref, pos_ref, sem):
+    n = own_ref.shape[0]
+    own = pltpu.make_async_copy(own_ref, q_ref.at[:n], sem)
+    own.start()
+    for i, ref in enumerate((rows_ref, other_rows_ref)):
+        part = slice(i * n, (i + 1) * n)
+        w_ref[:, part] = ref[1:2, :]
+        off_ref[:, part] = ref[0:1, :] * LOG2E - jnp.log2(ref[1:2, :])
+        pos_ref[:, part] = ref[2:3, :].astype(jnp.int32)
+    q_ref[n:, :] = other_ref[...]
+    qt_ref[:, n:] = other_ref[...].T
+    own.wait()
+    qt_ref[:, :n] = q_ref[:n, :].T
+
+
+def layout(queries, other_queries, rows, other_rows):
+    n, width = queries.shape
+    vmem = pl.BlockSpec(memory_space=pltpu.VMEM)
+    line = jax.ShapeDtypeStruct((1, 2 * n), F32)
+    return pl.pallas_call(
+        layout_kernel,
+        in_specs=[pl.BlockSpec(memory_space=pltpu.HBM)] + [vmem] * 3,
+        out_specs=[vmem] * 5,
+        out_shape=[
+            jax.ShapeDtypeStruct((2 * n, width), BF16),
+            jax.ShapeDtypeStruct((width, 2 * n), BF16),
+            line,
+            line,
+            jax.ShapeDtypeStruct((1, 2 * n), jnp.int32),
+        ],
+        scratch_shapes=[pltpu.SemaphoreType.DMA],
+        compiler_params=pltpu.CompilerParams(vmem_limit_bytes=VMEM_LIMIT),
+        name="layout",
+    )(pltpu.with_memory_space_constraint(queries, pltpu.HBM), other_queries, rows, other_rows)
+
+
 def kernel(sizes, side, split, *refs):
     n_x, n_y, n_z = sizes
     first, last = side == SIDES_IN_TURN[0], side == SIDES_IN_TURN[-1]
-    place_ref, xd_ref, yd_ref, off_ref, w_ref, pos_ref, ends_ref, *refs = refs
+    place_ref, xd_ref, yd_ref, q_ref, qt_ref, off_ref, w_ref, pos_ref, ends_ref, *refs = refs
     nq = off_ref.shape[1]
-    if first:
-        own_ref, other_ref, *refs = refs
-    else:
-        q_ref, qt_ref, gq_in, found_in, *refs = refs
+    if not first:
+        gq_in, found_in, *refs = refs
     half = xd_ref.shape[0]
     nd = 2 * half
     outs = nd // split
     gd_refs, refs = refs[:outs], refs[outs:]
     gq_ref, found_ref, *refs = refs
-    if first:
-        q_ref, qt_ref, *refs = refs
     dt_ref, id_ref, c_ref, gd_ref, sems = refs
 
-    if first:
-        own = pltpu.make_async_copy(own_ref, q_ref.at[: nq // 2], sems.at[nd // SUB])
-        own.start()
-        q_ref[nq // 2 :, :] = other_ref[...]
-        qt_ref[:, nq // 2 :] = other_ref[...].T
     if last:
         top = lax.broadcasted_iota(jnp.int32, found_ref.shape, 0) == 0
         found_ref[...] = jnp.where(top, ends_ref[...], 0.0)
@@ -73,9 +100,6 @@
         id_ref[block * piece : (block + 1) * piece, :] = row + base * piece
     for i, ref in enumerate((xd_ref, yd_ref)):
         dt_ref[:, i * half : (i + 1) * half] = ref[...].T
-    if first:
-        own.wait()
-        qt_ref[:, : nq // 2] = q_ref[: nq // 2, :].T
 
     def front(tile, slot):
         cols = pl.ds(pl.multiple_of(tile * QT, QT), QT)
@@ -132,22 +156,20 @@
     back(tiles - 1, 1, closing=True)
 
 
-def fused(side, split, place, x_docs, y_docs, off, w, pos, ends, extra, sizes):
-    nq = off.shape[1]
+def fused(side, split, place, x_docs, y_docs, asked, ends, sums, sizes):
+    nq = asked[0].shape[0]
     width = x_docs.shape[1]
     nd = 2 * x_docs.shape[0]
     vmem = pl.BlockSpec(memory_space=pltpu.VMEM)
     hbm = pl.BlockSpec(memory_space=pltpu.HBM)
     first, last = side == SIDES_IN_TURN[0], side == SIDES_IN_TURN[-1]
-    operands = [place, x_docs, y_docs, off, w, pos, ends, *extra]
+    operands = [place, x_docs, y_docs, *asked, ends, *sums]
     outs = nd // split
     out_shape = [pltpu.HBM((split, width), F32)] * outs
     out_shape += [jax.ShapeDtypeStruct((width, nq), F32), jax.ShapeDtypeStruct((8, QT if last else nq), F32)]
-    if first:
-        out_shape += [jax.ShapeDtypeStruct((nq, width), BF16), jax.ShapeDtypeStruct((width, nq), BF16)]
     return pl.pallas_call(
         functools.partial(kernel, sizes, side, split),
-        in_specs=[pl.BlockSpec(memory_space=pltpu.SMEM)] + [vmem] * 6 + [hbm if first else vmem] + [vmem] * (len(operands) - 8),
+        in_specs=[pl.BlockSpec(memory_space=pltpu.SMEM)] + [vmem] * (len(operands) - 1),
         out_specs=[hbm] * outs + [vmem] * (len(out_shape) - outs),
         out_shape=out_shape,
         scratch_shapes=[
@@ -155,7 +177,7 @@
             pltpu.VMEM((nd, 128), jnp.int32),
             pltpu.VMEM((2, nd, QT), BF16),
             pltpu.VMEM((nd, width), F32),
-            pltpu.SemaphoreType.DMA((nd // SUB + 1,)),
+            pltpu.SemaphoreType.DMA((nd // SUB,)),
         ],
         input_output_aliases={} if first else {9: outs},
         compiler_params=pltpu.CompilerParams(vmem_limit_bytes=VMEM_LIMIT),
@@ -176,11 +198,7 @@
     place = jnp.stack([lax.axis_index(X), lax.axis_index(Y), lax.axis_index("core")]).astype(jnp.int32)
 
     rows = jnp.stack([log_norms, weights, positives.astype(F32)])
-    rows = jnp.concatenate([rows, other_core(rows)], 1)
-    other_queries = other_core(queries)
-    w = rows[1:2]
-    off = rows[0:1] * LOG2E - jnp.log2(w)
-    pos = rows[2:3].astype(jnp.int32)
+    asked = layout(queries, other_core(queries), rows, other_core(rows))
 
     column = lax.all_to_all(jnp.broadcast_to(documents[None], (n_z, piece, width)), "z", 0, 0, tiled=True)
     x_part, y_part = column.reshape(2, n_z // 2 * piece, width)
@@ -192,17 +210,13 @@
     half = x_docs[0].shape[0]
     terms = {}
     ends = (weights * log_norms).reshape(-1, QT).sum(0)[None]
-    extra = (pltpu.with_memory_space_constraint(queries, pltpu.HBM), other_queries)
+    sums = ()
     for side in SIDES_IN_TURN:
         split = half // 2 if side == 2 else half
         outs = 2 * half // split
-        got = fused(side, split, place, x_docs[side], y_docs[side], off, w, pos, ends, extra, (n_x, n_y, n_z))
+        got = fused(side, split, place, x_docs[side], y_docs[side], asked, ends, sums, (n_x, n_y, n_z))
         terms[side] = got[:outs]
-        grad_q, found = got[outs : outs + 2]
-        layouts = got[outs + 2 :] or layouts
-        extra = (*layouts, grad_q, found)
-
-    lost = found + other_core(found)
+        sums = grad_q, lost = got[outs:]
 
     def ring(own_term, ahead, behind, far_a, far_b, axes):
         n = half // 2
@@ -224,12 +238,15 @@
     y_sum = sum(moved(y_total[i * n : (i + 1) * n], X, -s) for i, s in enumerate(SIDES))
     part = jnp.concatenate([x_sum[:n], y_sum]).reshape(n_z, piece, width)
     part = jnp.concatenate([part, jnp.broadcast_to(x_sum[n:][None], (n_z, 8, width))], 1)
-    part = lax.all_to_all(part, "z", 0, 0, tiled=True).sum(0)
+    part = lax.all_to_all(part, "z", 0, 0, tiled=True)
+    part = part.sum(0)
     grad_documents = (part[:piece] * 0.0625).astype(BF16)
-    loss = jnp.sum(part[piece:]) / total_q
-
-    grad_q = grad_q[:, :own] + other_core(grad_q[:, own:])
-    grad_queries = (grad_q.T * 0.0625).astype(BF16)
+    lost = jnp.broadcast_to(jnp.sum(part[piece:]), (8, 128))
+    loss = (lost + other_core(lost))[0, 0] / total_q
+
+    other_grad = grad_q[:, own:]
+    other_grad = other_core(other_grad)
+    grad_queries = ((grad_q[:, :own] + other_grad).T * 0.0625).astype(BF16)
     return (grad_queries, grad_documents, loss)
 
 

time: 132 us -> 132 us (level)
  the two profiles are of different devices: /device:TPU:32 before, /device:TPU:7 now
where the time goes in v2:
time: 132 us
  starting transfers between devices  55.2 us (42%)
  waiting for transfers between devices  35.1 us (27%)
  Pallas kernels  26.1 us (20%)
  other arithmetic  7.1 us (5%)
  local copies, waits for them, and re-layouts  5.23 us (4%)
  between operations  2.79 us (2%)
    ppermute x27, starting transfers between devices, moved(): lax.ppermute(array, axes, [(i, (i + distance) % peers) for i in range(pee...  29.5 us
    pallas_call x4, Pallas kernels, fused(): pl.pallas_call(functools.partial(kernel, sizes, side, split), in_specs=[p...  24.9 us
    ppermute x27, waiting for transfers between devices, moved(): lax.ppermute(array, axes, [(i, (i + distance) % peers) for i in range(pee...  20.1 us
    ppermute x4, starting transfers between devices, other_core(): return lax.ppermute(array, 'core', [(0, 1), (1, 0)])  14.1 us
    all_to_all x1, waiting for transfers between devices, on_device(): part = lax.all_to_all(part, 'z', 0, 0, tiled=True)  10.4 us
    all_to_all x1, starting transfers between devices, on_device(): lax.all_to_all(jnp.broadcast_to(documents[None], (n_z, piece, width)), 'z...  8.19 us
    all_to_all x1, waiting for transfers between devices, on_device(): lax.all_to_all(jnp.broadcast_to(documents[None], (n_z, piece, width)), 'z...  4.46 us
    all_to_all x1, starting transfers between devices, on_device(): part = lax.all_to_all(part, 'z', 0, 0, tiled=True)  3.43 us
  transfers between devices with their start and end apart: 33, of which 11 were waited for; matrix products, arithmetic and copies ran while one was open for 6% of the time, Pallas kernels for 20%

profile of v2, /device:TPU:7, one launch (start us, length us, event | category | flops | bytes accessed | tf_op | source)
XLA Modules:
  0.0 131.6 jit_solution(7939784259991409848)
XLA Ops:
  0.6 1.4 %broadcast_in_dim.8 = bf16[8,32,256]{2,1,0:T(8,128)(2,1)} broadcast(bf16[32,256]{1,0:T(8,128)(2,1)} %param.6), dimensions={1,2} | broadcast | bytes 147456 | tf_op jit(solution)/shard_map/broadcast_in_dim | solution.py:203
  2.0 8.2 %all-to-all-start = ((bf16[8,32,256]{2,1,0:T(8,128)(2,1)}), bf16[8,32,256]{2,1,0:T(8,128)(2,1)S(1)}, u32[]{:S(2)}, u32[]{:S(2)}) async-start(bf16[8,32,256]{2,1,0:T(8,128)(2,1)} %broadcast_in_dim.8), calls=%async_computation | async-start | bytes 262144 | tf_op jit(solution)/shard_map/all_to_all | solution.py:203
  10.2 0.7 convert_element_type.12
  10.9 0.7 pad_maximum_fusion.12.rows_ref
  11.6 1.0 collective-permute-start.9
  12.7 0.7 mul.20
  13.5 4.5 %all-to-all-done = bf16[8,32,256]{2,1,0:T(8,128)(2,1)S(1)} async-done(((bf16[8,32,256]{2,1,0:T(8,128)(2,1)}), bf16[8,32,256]{2,1,0:T(8,128)(2,1)S(1)}, u32[]{:S(2)}, u32[]{:S(2)}) %all-to-all-start) | async-done | bytes 131104 | tf_op jit(solution)/shard_map/all_to_all | solution.py:203
  18.0 1.2 collective-permute-start.6
  19.2 2.7 %collective-permute-start.4 = (bf16[128,256]{1,0:T(8,128)(2,1)S(1)}, bf16[128,256]{1,0:T(8,128)(2,1)S(1)}, u32[]{:S(2)}, u32[]{:S(2)}) collective-permute-start(bf16[128,256]{1,0:T(8,128)(2,1)S(1)} %bitcast.24), channel_id=1, source_target_pairs={{0,1},{1,16},{16,17},{17,0},{2,3},{3,18},{18,19},{19,2},{4,5},{5,2... | collective-permute-start | bytes 196616 | tf_op jit(solution)/shard_map/ppermute | solution.py:34
  21.9 0.7 collective-permute-done.6
  22.7 2.9 %collective-permute-start.2 = (bf16[128,256]{1,0:T(8,128)(2,1)S(1)}, bf16[128,256]{1,0:T(8,128)(2,1)S(1)}, u32[]{:S(2)}, u32[]{:S(2)}) collective-permute-start(bf16[128,256]{1,0:T(8,128)(2,1)S(1)} %bitcast.18), channel_id=1, source_target_pairs={{0,4},{2,6},{4,0},{6,2},{1,5},{3,7},{5,1},{7,3},{8,12},{10,14},{12... | collective-permute-start | bytes 196616 | tf_op jit(solution)/shard_map/ppermute | solution.py:34
  25.6 0.8 collective-permute-start.1
  26.4 0.7 collective-permute-start
  27.3 2.7 %collective-permute-start.13 = (bf16[512,256]{1,0:T(8,128)(2,1)S(1)}, bf16[512,256]{1,0:T(8,128)(2,1)S(1)}, u32[]{:S(2)}, u32[]{:S(2)}) collective-permute-start(bf16[512,256]{1,0:T(8,128)(2,1)S(1)} %pad_maximum_fusion.10.refs_2_), channel_id=1, source_target_pairs={{0,6},{2,0},{4,2},{6,4},{1,7},{3,1},{5,3},{7,5},{8,14},{10,8},{12,... | collective-permute-start | bytes 786440 | tf_op jit(solution)/shard_map/ppermute | solution.py:34
  30.0 0.4 collective-permute-start.11
  30.4 1.1 collective-permute-done
  31.5 0.6 collective-permute-start.12
  32.2 1.1 collective-permute-start.10
  33.2 1.3 layout.1
  34.5 6.2 %fused.4 = (f32[512,256]{1,0:T(8,128)}, f32[512,256]{1,0:T(8,128)}, f32[256,2048]{1,0:T(8,128)S(1)}, f32[8,2048]{1,0:T(8,128)S(1)}) custom-call(s32[3]{0:T(128)S(1)} %pad_add_fusion.refs_0_, bf16[512,256]{1,0:T(8,128)(2,1)S(1)} %pad_maximum_fusion.9.refs_1_, bf16[512,256]{1,0:T(8,128)(2,1)S(1)} %pad_maximum_fusion.10.refs_2_, ...), custom_call_target="tpu_custom_call" | custom-call | flops 3221225472 | bytes 8388608 | tf_op jit(solution)/shard_map/fused/pallas_call | solution.py:170
  40.7 1.9 %collective-permute-start.3 = (bf16[512,256]{1,0:T(8,128)(2,1)S(1)}, bf16[512,256]{1,0:T(8,128)(2,1)S(1)}, u32[]{:S(2)}, u32[]{:S(2)}) collective-permute-start(bf16[512,256]{1,0:T(8,128)(2,1)S(1)} %pad_maximum_fusion.9.refs_1_), channel_id=1, source_target_pairs={{0,1},{1,16},{16,17},{17,0},{2,3},{3,18},{18,19},{19,2},{4,5},{5,2... | collective-permute-start | bytes 786440 | tf_op jit(solution)/shard_map/ppermute | solution.py:34
  42.6 6.2 %fused.5 = (f32[512,256]{1,0:T(8,128)}, f32[512,256]{1,0:T(8,128)}, f32[256,2048]{1,0:T(8,128)S(1)}, f32[8,2048]{1,0:T(8,128)S(1)}) custom-call(s32[3]{0:T(128)S(1)} %pad_add_fusion.refs_0_, bf16[512,256]{1,0:T(8,128)(2,1)S(1)} %collective-permute-done.12.refs_1_, ...), custom_call_target="tpu_custom_call", output_to_operand_aliasing={{2}: (9, {})} | custom-call | flops 3221225472 | bytes 8388608 | tf_op jit(solution)/shard_map/fused/pallas_call | solution.py:170
  48.8 6.2 %fused.6 = (f32[256,256]{1,0:T(8,128)}, f32[256,256]{1,0:T(8,128)}, f32[256,256]{1,0:T(8,128)}, f32[256,256]{1,0:T(8,128)}, f32[256,2048]{1,0:T(8,128)S(1)}, /*index=5*/f32[8,2048]{1,0:T(8,128)S(1)}) custom-call(s32[3]{0:T(128)S(1)} %pad_add_fusion.refs_0_, bf16[512,256]{1,0:T(8,128)(2,1)S(1)} %collective-permute-done.10.refs_1_, ...), custom_call_target="tpu_custom_call", output_to_operand_aliasing={{4}: (9, {})} | custom-call | flops 3221225472 | bytes 8388608 | tf_op jit(solution)/shard_map/fused/pallas_call | solution.py:170
  55.2 2.6 %collective-permute-start.17 = (f32[256,256]{1,0:T(8,128)}, f32[256,256]{1,0:T(8,128)S(1)}, u32[]{:S(2)}, u32[]{:S(2)}) collective-permute-start(f32[256,256]{1,0:T(8,128)} %get-tuple-element.43), channel_id=1, source_target_pairs={{0,1},{1,16},{16,17},{17,0},{2,3},{3,18},{18,19},{19,2},{4,5},{5,2... | collective-permute-start | bytes 786440 | tf_op jit(solution)/shard_map/ppermute | solution.py:34
  57.8 2.7 %collective-permute-start.23 = (f32[256,256]{1,0:T(8,128)}, f32[256,256]{1,0:T(8,128)S(1)}, u32[]{:S(2)}, u32[]{:S(2)}) collective-permute-start(f32[256,256]{1,0:T(8,128)} %get-tuple-element.46), channel_id=1, source_target_pairs={{0,6},{2,0},{4,2},{6,4},{1,7},{3,1},{5,3},{7,5},{8,14},{10,8},{12,... | collective-permute-start | bytes 786440 | tf_op jit(solution)/shard_map/ppermute | solution.py:34
  60.5 6.3 %fused.7 = (f32[512,256]{1,0:T(8,128)}, f32[512,256]{1,0:T(8,128)}, f32[256,2048]{1,0:T(8,128)S(1)}, f32[8,256]{1,0:T(8,128)S(1)}) custom-call(s32[3]{0:T(128)S(1)} %pad_add_fusion.refs_0_, bf16[512,256]{1,0:T(8,128)(2,1)S(1)} %collective-permute-done.3.refs_1_, ...), custom_call_target="tpu_custom_call", output_to_operand_aliasing={{2}: (9, {})} | custom-call | flops 3221225472 | bytes 8388608 | tf_op jit(solution)/shard_map/fused/pallas_call | solution.py:170
  67.3 0.5 copy-done.3
  67.9 2.9 %collective-permute-start.24 = (f32[512,256]{1,0:T(8,128)S(1)}, f32[512,256]{1,0:T(8,128)S(1)}, u32[]{:S(2)}, u32[]{:S(2)}) collective-permute-start(f32[512,256]{1,0:T(8,128)S(1)} %pad_maximum_fusion.2), channel_id=1, source_target_pairs={{0,6},{2,0},{4,2},{6,4},{1,7},{3,1},{5,3},{7,5},{8,14},{10,8},{12,... | collective-permute-start | bytes 1572872 | tf_op jit(solution)/shard_map/ppermute | solution.py:34
  71.2 2.7 %collective-permute-start.18 = (f32[520,256]{1,0:T(8,128)S(1)}, f32[520,256]{1,0:T(8,128)S(1)}, u32[]{:S(2)}, u32[]{:S(2)}) collective-permute-start(f32[520,256]{1,0:T(8,128)S(1)} %get-tuple-element.76), channel_id=1, source_target_pairs={{0,1},{1,16},{16,17},{17,0},{2,3},{3,18},{18,19},{19,2},{4,5},{5,2... | collective-permute-start | bytes 1597448 | tf_op jit(solution)/shard_map/ppermute | solution.py:34
  73.9 1.1 slice.84
  74.9 4.1 %collective-permute-done.26 = f32[512,256]{1,0:T(8,128)S(1)} collective-permute-done((f32[512,256]{1,0:T(8,128)S(1)}, f32[512,256]{1,0:T(8,128)S(1)}, u32[]{:S(2)}, u32[]{:S(2)}) %collective-permute-start.26) | collective-permute-done | bytes 524320 | tf_op jit(solution)/shard_map/ppermute | solution.py:34
  79.1 11.5 %collective-permute-start.14 = (f32[256,1024]{1,0:T(8,128)}, f32[256,1024]{1,0:T(8,128)}, u32[]{:S(2)}, u32[]{:S(2)}) collective-permute-start(f32[256,1024]{1,0:T(8,128)} %slice.84), channel_id=1, source_target_pairs={{0,8},{8,0},{1,9},{9,1},{2,10},{10,2},{3,11},{11,3},{4,12},{12,4},... | collective-permute-start | bytes 3145736 | tf_op jit(solution)/shard_map/ppermute | solution.py:27
  90.8 1.2 collective-permute-start.29
  92.1 2.0 %collective-permute-start.28 = (f32[128,256]{1,0:T(8,128)S(1)}, f32[128,256]{1,0:T(8,128)S(1)}, u32[]{:S(2)}, u32[]{:S(2)}) collective-permute-start(f32[128,256]{1,0:T(8,128)S(1)} %get-tuple-element.57), channel_id=1, source_target_pairs={{0,1},{1,16},{16,17},{17,0},{2,3},{3,18},{18,19},{19,2},{4,5},{5,2... | collective-permute-start | bytes 393224 | tf_op jit(solution)/shard_map/ppermute | solution.py:34
  94.4 4.1 %collective-permute-done.27 = f32[128,256]{1,0:T(8,128)S(1)} collective-permute-done((f32[128,256]{1,0:T(8,128)S(1)}, f32[128,256]{1,0:T(8,128)S(1)}, u32[]{:S(2)}, u32[]{:S(2)}) %collective-permute-start.27) | collective-permute-done | bytes 131104 | tf_op jit(solution)/shard_map/ppermute | solution.py:34
  98.5 1.5 %collective-permute-done.28 = f32[128,256]{1,0:T(8,128)S(1)} collective-permute-done((f32[128,256]{1,0:T(8,128)S(1)}, f32[128,256]{1,0:T(8,128)S(1)}, u32[]{:S(2)}, u32[]{:S(2)}) %collective-permute-start.28) | collective-permute-done | bytes 131104 | tf_op jit(solution)/shard_map/ppermute | solution.py:34
  100.0 7.9 %collective-permute-done.21 = f32[136,256]{1,0:T(8,128)S(1)} collective-permute-done((f32[136,256]{1,0:T(8,128)S(1)}, f32[136,256]{1,0:T(8,128)S(1)}, u32[]{:S(2)}, u32[]{:S(2)}) %collective-permute-start.21) | collective-permute-done | bytes 139296 | tf_op jit(solution)/shard_map/ppermute | solution.py:34
  108.1 0.8 pad_maximum_fusion.4
  108.9 3.4 %all-to-all-start.1 = ((f32[8,40,256]{2,1,0:T(8,128)}), f32[8,40,256]{2,1,0:T(8,128)S(1)}, u32[]{:S(2)}, u32[]{:S(2)}) async-start(f32[8,40,256]{2,1,0:T(8,128)} %pad_maximum_fusion.4), calls=%async_computation.1 | async-start | bytes 655360 | tf_op jit(solution)/shard_map/all_to_all | solution.py:241
  112.3 1.4 %fusion = bf16[1024,256]{0,1:T(8,128)(2,1)S(1)} fusion(f32[256,1024]{1,0:T(8,128)} %collective-permute-done.14, f32[256,2048]{1,0:T(8,128)S(1)} %get-tuple-element.37), kind=kLoop, calls=%fused_computation.3 | loop fusion | flops 786432 | bytes 2621440 | tf_op jit(solution)/shard_map/convert_element_type | solution.py:249
  113.8 1.0 copy.12
  114.8 10.4 %all-to-all-done.1 = f32[8,40,256]{2,1,0:T(8,128)S(1)} async-done(((f32[8,40,256]{2,1,0:T(8,128)}), f32[8,40,256]{2,1,0:T(8,128)S(1)}, u32[]{:S(2)}, u32[]{:S(2)}) %all-to-all-start.1) | async-done | bytes 327712 | tf_op jit(solution)/shard_map/all_to_all | solution.py:241
  125.2 0.6 slice_reduce_fusion
  125.8 0.6 broadcast_in_dim.21
  126.4 1.4 %collective-permute-start.30 = (f32[8,128]{1,0:T(8,128)S(1)}, f32[8,128]{1,0:T(8,128)S(1)}, u32[]{:S(2)}, u32[]{:S(2)}) collective-permute-start(f32[8,128]{1,0:T(8,128)S(1)} %broadcast_in_dim.21), channel_id=1, source_target_pairs={{0,8},{8,0},{1,9},{9,1},{2,10},{10,2},{3,11},{11,3},{4,12},{12,4},... | collective-permute-start | bytes 12296 | tf_op jit(solution)/shard_map/ppermute | solution.py:27
  127.8 0.6 fusion.6
  128.6 0.6 broadcast_add_fusion
  129.3 0.5 slice.109
  (74 shorter events, 2.5 us)
Async XLA Ops:
  2.0 15.9 %all-to-all-start = ((bf16[8,32,256]{2,1,0:T(8,128)(2,1)}), bf16[8,32,256]{2,1,0:T(8,128)(2,1)S(1)}, u32[]{:S(2)}, u32[]{:S(2)}) async-start(bf16[8,32,256]{2,1,0:T(8,128)(2,1)} %broadcast_in_dim.8), calls=%async_computation | async-start | bytes 262144 | tf_op jit(solution)/shard_map/all_to_all | solution.py:203
  11.6 19.9 %collective-permute-start.9 = (f32[3,1024]{1,0:T(4,128)S(1)}, f32[3,1024]{1,0:T(4,128)S(1)}, u32[]{:S(2)}, u32[]{:S(2)}) collective-permute-start(f32[3,1024]{1,0:T(4,128)S(1)} %pad_maximum_fusion.12.rows_ref), channel_id=1, source_target_pairs={{0,8},{8,0},{1,9},{9,1},{2,10},{10,2},{3,11},{11,3},{4,12},{12,4},... | collective-permute-start | bytes 36872 | tf_op jit(solution)/shard_map/ppermute | solution.py:27
  12.6 19.5 %collective-permute-start.8 = (bf16[1024,256]{1,0:T(8,128)(2,1)}, bf16[1024,256]{1,0:T(8,128)(2,1)S(1)}, u32[]{:S(2)}, u32[]{:S(2)}) collective-permute-start(bf16[1024,256]{1,0:T(8,128)(2,1)} %own_ref.1), channel_id=1, source_target_pairs={{0,8},{8,0},{1,9},{9,1},{2,10},{10,2},{3,11},{11,3},{4,12},{12,4},... | collective-permute-start | bytes 1572872 | tf_op jit(solution)/shard_map/ppermute | solution.py:27
  18.0 4.7 %collective-permute-start.6 = (bf16[128,256]{1,0:T(8,128)(2,1)S(1)}, bf16[128,256]{1,0:T(8,128)(2,1)S(1)}, u32[]{:S(2)}, u32[]{:S(2)}) collective-permute-start(bf16[128,256]{1,0:T(8,128)(2,1)S(1)} %bitcast.22), channel_id=1, source_target_pairs={{0,16},{1,17},{16,0},{17,1},{2,18},{3,19},{18,2},{19,3},{4,20},{5,... | collective-permute-start | bytes 196616 | tf_op jit(solution)/shard_map/ppermute | solution.py:34
  19.2 6.4 %collective-permute-start.5 = (bf16[128,256]{1,0:T(8,128)(2,1)S(1)}, bf16[128,256]{1,0:T(8,128)(2,1)S(1)}, u32[]{:S(2)}, u32[]{:S(2)}) collective-permute-start(bf16[128,256]{1,0:T(8,128)(2,1)S(1)} %bitcast.23), channel_id=1, source_target_pairs={{0,17},{1,0},{16,1},{17,16},{2,19},{3,2},{18,3},{19,18},{4,21},{5,... | collective-permute-start | bytes 196616 | tf_op jit(solution)/shard_map/ppermute | solution.py:34
  19.2 7.2 %collective-permute-start.4 = (bf16[128,256]{1,0:T(8,128)(2,1)S(1)}, bf16[128,256]{1,0:T(8,128)(2,1)S(1)}, u32[]{:S(2)}, u32[]{:S(2)}) collective-permute-start(bf16[128,256]{1,0:T(8,128)(2,1)S(1)} %bitcast.24), channel_id=1, source_target_pairs={{0,1},{1,16},{16,17},{17,0},{2,3},{3,18},{18,19},{19,2},{4,5},{5,2... | collective-permute-start | bytes 196616 | tf_op jit(solution)/shard_map/ppermute | solution.py:34
  22.7 4.6 %collective-permute-start.2 = (bf16[128,256]{1,0:T(8,128)(2,1)S(1)}, bf16[128,256]{1,0:T(8,128)(2,1)S(1)}, u32[]{:S(2)}, u32[]{:S(2)}) collective-permute-start(bf16[128,256]{1,0:T(8,128)(2,1)S(1)} %bitcast.18), channel_id=1, source_target_pairs={{0,4},{2,6},{4,0},{6,2},{1,5},{3,7},{5,1},{7,3},{8,12},{10,14},{12... | collective-permute-start | bytes 196616 | tf_op jit(solution)/shard_map/ppermute | solution.py:34
  25.6 4.4 %collective-permute-start.1 = (bf16[128,256]{1,0:T(8,128)(2,1)S(1)}, bf16[128,256]{1,0:T(8,128)(2,1)S(1)}, u32[]{:S(2)}, u32[]{:S(2)}) collective-permute-start(bf16[128,256]{1,0:T(8,128)(2,1)S(1)} %bitcast.19), channel_id=1, source_target_pairs={{0,6},{2,0},{4,2},{6,4},{1,7},{3,1},{5,3},{7,5},{8,14},{10,8},{12,... | collective-permute-start | bytes 196616 | tf_op jit(solution)/shard_map/ppermute | solution.py:34
  26.4 5.1 %collective-permute-start = (bf16[128,256]{1,0:T(8,128)(2,1)S(1)}, bf16[128,256]{1,0:T(8,128)(2,1)S(1)}, u32[]{:S(2)}, u32[]{:S(2)}) collective-permute-start(bf16[128,256]{1,0:T(8,128)(2,1)S(1)} %bitcast.20), channel_id=1, source_target_pairs={{0,2},{2,4},{4,6},{6,0},{1,3},{3,5},{5,7},{7,1},{8,10},{10,12},{12... | collective-permute-start | bytes 196616 | tf_op jit(solution)/shard_map/ppermute | solution.py:34
  27.3 13.4 %collective-permute-start.13 = (bf16[512,256]{1,0:T(8,128)(2,1)S(1)}, bf16[512,256]{1,0:T(8,128)(2,1)S(1)}, u32[]{:S(2)}, u32[]{:S(2)}) collective-permute-start(bf16[512,256]{1,0:T(8,128)(2,1)S(1)} %pad_maximum_fusion.10.refs_2_), channel_id=1, source_target_pairs={{0,6},{2,0},{4,2},{6,4},{1,7},{3,1},{5,3},{7,5},{8,14},{10,8},{12,... | collective-permute-start | bytes 786440 | tf_op jit(solution)/shard_map/ppermute | solution.py:34
  30.0 18.7 %collective-permute-start.11 = (bf16[512,256]{1,0:T(8,128)(2,1)S(1)}, bf16[512,256]{1,0:T(8,128)(2,1)S(1)}, u32[]{:S(2)}, u32[]{:S(2)}) collective-permute-start(bf16[512,256]{1,0:T(8,128)(2,1)S(1)} %pad_maximum_fusion.10.refs_2_), channel_id=1, source_target_pairs={{0,4},{2,6},{4,0},{6,2},{1,5},{3,7},{5,1},{7,3},{8,12},{10,14},{12... | collective-permute-start | bytes 786440 | tf_op jit(solution)/shard_map/ppermute | solution.py:34
  31.5 28.9 %collective-permute-start.7 = (bf16[512,256]{1,0:T(8,128)(2,1)S(1)}, bf16[512,256]{1,0:T(8,128)(2,1)S(1)}, u32[]{:S(2)}, u32[]{:S(2)}) collective-permute-start(bf16[512,256]{1,0:T(8,128)(2,1)S(1)} %pad_maximum_fusion.10.refs_2_), channel_id=1, source_target_pairs={{0,2},{2,4},{4,6},{6,0},{1,3},{3,5},{5,7},{7,1},{8,10},{10,12},{12... | collective-permute-start | bytes 786440 | tf_op jit(solution)/shard_map/ppermute | solution.py:34
  31.5 11.0 %collective-permute-start.12 = (bf16[512,256]{1,0:T(8,128)(2,1)S(1)}, bf16[512,256]{1,0:T(8,128)(2,1)S(1)}, u32[]{:S(2)}, u32[]{:S(2)}) collective-permute-start(bf16[512,256]{1,0:T(8,128)(2,1)S(1)} %pad_maximum_fusion.9.refs_1_), channel_id=1, source_target_pairs={{0,17},{1,0},{16,1},{17,16},{2,19},{3,2},{18,3},{19,18},{4,21},{5,... | collective-permute-start | bytes 786440 | tf_op jit(solution)/shard_map/ppermute | solution.py:34
  32.2 16.6 %collective-permute-start.10 = (bf16[512,256]{1,0:T(8,128)(2,1)S(1)}, bf16[512,256]{1,0:T(8,128)(2,1)S(1)}, u32[]{:S(2)}, u32[]{:S(2)}) collective-permute-start(bf16[512,256]{1,0:T(8,128)(2,1)S(1)} %pad_maximum_fusion.9.refs_1_), channel_id=1, source_target_pairs={{0,16},{1,17},{16,0},{17,1},{2,18},{3,19},{18,2},{19,3},{4,20},{5,... | collective-permute-start | bytes 786440 | tf_op jit(solution)/shard_map/ppermute | solution.py:34
  40.7 19.8 %collective-permute-start.3 = (bf16[512,256]{1,0:T(8,128)(2,1)S(1)}, bf16[512,256]{1,0:T(8,128)(2,1)S(1)}, u32[]{:S(2)}, u32[]{:S(2)}) collective-permute-start(bf16[512,256]{1,0:T(8,128)(2,1)S(1)} %pad_maximum_fusion.9.refs_1_), channel_id=1, source_target_pairs={{0,1},{1,16},{16,17},{17,0},{2,3},{3,18},{18,19},{19,2},{4,5},{5,2... | collective-permute-start | bytes 786440 | tf_op jit(solution)/shard_map/ppermute | solution.py:34
  55.0 15.8 %collective-permute-start.15 = (f32[256,256]{1,0:T(8,128)}, f32[256,256]{1,0:T(8,128)S(1)}, u32[]{:S(2)}, u32[]{:S(2)}) collective-permute-start(f32[256,256]{1,0:T(8,128)} %get-tuple-element.40), channel_id=1, source_target_pairs={{0,17},{1,0},{16,1},{17,16},{2,19},{3,2},{18,3},{19,18},{4,21},{5,... | collective-permute-start | bytes 786440 | tf_op jit(solution)/shard_map/ppermute | solution.py:34
  55.2 15.7 %collective-permute-start.17 = (f32[256,256]{1,0:T(8,128)}, f32[256,256]{1,0:T(8,128)S(1)}, u32[]{:S(2)}, u32[]{:S(2)}) collective-permute-start(f32[256,256]{1,0:T(8,128)} %get-tuple-element.43), channel_id=1, source_target_pairs={{0,1},{1,16},{16,17},{17,0},{2,3},{3,18},{18,19},{19,2},{4,5},{5,2... | collective-permute-start | bytes 786440 | tf_op jit(solution)/shard_map/ppermute | solution.py:34
  57.8 9.5 %collective-permute-start.23 = (f32[256,256]{1,0:T(8,128)}, f32[256,256]{1,0:T(8,128)S(1)}, u32[]{:S(2)}, u32[]{:S(2)}) collective-permute-start(f32[256,256]{1,0:T(8,128)} %get-tuple-element.46), channel_id=1, source_target_pairs={{0,6},{2,0},{4,2},{6,4},{1,7},{3,1},{5,3},{7,5},{8,14},{10,8},{12,... | collective-permute-start | bytes 786440 | tf_op jit(solution)/shard_map/ppermute | solution.py:34
  60.4 6.6 %collective-permute-start.25 = (f32[256,256]{1,0:T(8,128)}, f32[256,256]{1,0:T(8,128)S(1)}, u32[]{:S(2)}, u32[]{:S(2)}) collective-permute-start(f32[256,256]{1,0:T(8,128)} %get-tuple-element.48), channel_id=1, source_target_pairs={{0,2},{2,4},{4,6},{6,0},{1,3},{3,5},{5,7},{7,1},{8,10},{10,12},{12... | collective-permute-start | bytes 786440 | tf_op jit(solution)/shard_map/ppermute | solution.py:34
  60.4 6.6 %copy-start.1 = (f32[512,256]{1,0:T(8,128)S(1)}, f32[512,256]{1,0:T(8,128)}, u32[]{:S(2)}) copy-start(f32[512,256]{1,0:T(8,128)} %get-tuple-element.47) | copy-start | bytes 1572868
  66.7 1.0 copy-start.3
  67.1 3.8 %copy-start.2 = (f32[512,256]{1,0:T(8,128)S(1)}, f32[512,256]{1,0:T(8,128)}, u32[]{:S(2)}) copy-start(f32[512,256]{1,0:T(8,128)} %get-tuple-element.39) | copy-start | bytes 1572868
  67.2 3.7 %copy-start = (f32[512,256]{1,0:T(8,128)S(1)}, f32[512,256]{1,0:T(8,128)}, u32[]{:S(2)}) copy-start(f32[512,256]{1,0:T(8,128)} %get-tuple-element.42) | copy-start | bytes 1572868
  67.2 11.9 %collective-permute-start.26 = (f32[512,256]{1,0:T(8,128)S(1)}, f32[512,256]{1,0:T(8,128)S(1)}, u32[]{:S(2)}, u32[]{:S(2)}) collective-permute-start(f32[512,256]{1,0:T(8,128)S(1)} %pad_maximum_fusion.3), channel_id=1, source_target_pairs={{0,2},{2,4},{4,6},{6,0},{1,3},{3,5},{5,7},{7,1},{8,10},{10,12},{12... | collective-permute-start | bytes 1572872 | tf_op jit(solution)/shard_map/ppermute | solution.py:34
  67.9 22.7 %collective-permute-start.24 = (f32[512,256]{1,0:T(8,128)S(1)}, f32[512,256]{1,0:T(8,128)S(1)}, u32[]{:S(2)}, u32[]{:S(2)}) collective-permute-start(f32[512,256]{1,0:T(8,128)S(1)} %pad_maximum_fusion.2), channel_id=1, source_target_pairs={{0,6},{2,0},{4,2},{6,4},{1,7},{3,1},{5,3},{7,5},{8,14},{10,8},{12,... | collective-permute-start | bytes 1572872 | tf_op jit(solution)/shard_map/ppermute | solution.py:34
  71.0 19.6 %copy-start.5 = (f32[512,256]{1,0:T(8,128)S(1)}, f32[512,256]{1,0:T(8,128)}, u32[]{:S(2)}) copy-start(f32[512,256]{1,0:T(8,128)} %get-tuple-element.44) | copy-start | bytes 1572868
  71.1 19.7 %collective-permute-start.16 = (f32[520,256]{1,0:T(8,128)S(1)}, f32[520,256]{1,0:T(8,128)S(1)}, u32[]{:S(2)}, u32[]{:S(2)}) collective-permute-start(f32[520,256]{1,0:T(8,128)S(1)} %get-tuple-element.75), channel_id=1, source_target_pairs={{0,17},{1,0},{16,1},{17,16},{2,19},{3,2},{18,3},{19,18},{4,21},{5,... | collective-permute-start | bytes 1597448 | tf_op jit(solution)/shard_map/ppermute | solution.py:34
  71.2 20.9 %collective-permute-start.18 = (f32[520,256]{1,0:T(8,128)S(1)}, f32[520,256]{1,0:T(8,128)S(1)}, u32[]{:S(2)}, u32[]{:S(2)}) collective-permute-start(f32[520,256]{1,0:T(8,128)S(1)} %get-tuple-element.76), channel_id=1, source_target_pairs={{0,1},{1,16},{16,17},{17,0},{2,3},{3,18},{18,19},{19,2},{4,5},{5,2... | collective-permute-start | bytes 1597448 | tf_op jit(solution)/shard_map/ppermute | solution.py:34
  73.8 20.4 %collective-permute-start.19 = (f32[8,256]{1,0:T(8,128)S(1)}, f32[8,256]{1,0:T(8,128)S(1)}, u32[]{:S(2)}, u32[]{:S(2)}) collective-permute-start(f32[8,256]{1,0:T(8,128)S(1)} %get-tuple-element.41), channel_id=1, source_target_pairs={{0,16},{1,17},{16,0},{17,1},{2,18},{3,19},{18,2},{19,3},{4,20},{5,... | collective-permute-start | bytes 24584 | tf_op jit(solution)/shard_map/ppermute | solution.py:34
  73.9 20.2 %copy-start.4 = (f32[512,256]{1,0:T(8,128)S(1)}, f32[512,256]{1,0:T(8,128)}, u32[]{:S(2)}) copy-start(f32[512,256]{1,0:T(8,128)} %get-tuple-element.38) | copy-start | bytes 1572868
  79.1 33.2 %collective-permute-start.14 = (f32[256,1024]{1,0:T(8,128)}, f32[256,1024]{1,0:T(8,128)}, u32[]{:S(2)}, u32[]{:S(2)}) collective-permute-start(f32[256,1024]{1,0:T(8,128)} %slice.84), channel_id=1, source_target_pairs={{0,8},{8,0},{1,9},{9,1},{2,10},{10,2},{3,11},{11,3},{4,12},{12,4},... | collective-permute-start | bytes 3145736 | tf_op jit(solution)/shard_map/ppermute | solution.py:27
  90.7 7.7 %collective-permute-start.27 = (f32[128,256]{1,0:T(8,128)S(1)}, f32[128,256]{1,0:T(8,128)S(1)}, u32[]{:S(2)}, u32[]{:S(2)}) collective-permute-start(f32[128,256]{1,0:T(8,128)S(1)} %get-tuple-element.55), channel_id=1, source_target_pairs={{0,17},{1,0},{16,1},{17,16},{2,19},{3,2},{18,3},{19,18},{4,21},{5,... | collective-permute-start | bytes 393224 | tf_op jit(solution)/shard_map/ppermute | solution.py:34
  90.8 7.6 %collective-permute-start.29 = (f32[128,256]{1,0:T(8,128)S(1)}, f32[128,256]{1,0:T(8,128)S(1)}, u32[]{:S(2)}, u32[]{:S(2)}) collective-permute-start(f32[128,256]{1,0:T(8,128)S(1)} %get-tuple-element.56), channel_id=1, source_target_pairs={{0,16},{1,17},{16,0},{17,1},{2,18},{3,19},{18,2},{19,3},{4,20},{5,... | collective-permute-start | bytes 393224 | tf_op jit(solution)/shard_map/ppermute | solution.py:34
  92.1 7.9 %collective-permute-start.28 = (f32[128,256]{1,0:T(8,128)S(1)}, f32[128,256]{1,0:T(8,128)S(1)}, u32[]{:S(2)}, u32[]{:S(2)}) collective-permute-start(f32[128,256]{1,0:T(8,128)S(1)} %get-tuple-element.57), channel_id=1, source_target_pairs={{0,1},{1,16},{16,17},{17,0},{2,3},{3,18},{18,19},{19,2},{4,5},{5,2... | collective-permute-start | bytes 393224 | tf_op jit(solution)/shard_map/ppermute | solution.py:34
  94.3 5.7 %collective-permute-start.20 = (f32[136,256]{1,0:T(8,128)S(1)}, f32[136,256]{1,0:T(8,128)S(1)}, u32[]{:S(2)}, u32[]{:S(2)}) collective-permute-start(f32[136,256]{1,0:T(8,128)S(1)} %get-tuple-element.72), channel_id=1, source_target_pairs={{0,6},{2,0},{4,2},{6,4},{1,7},{3,1},{5,3},{7,5},{8,14},{10,8},{12,... | collective-permute-start | bytes 417800 | tf_op jit(solution)/shard_map/ppermute | solution.py:34
  98.5 9.5 %collective-permute-start.21 = (f32[136,256]{1,0:T(8,128)S(1)}, f32[136,256]{1,0:T(8,128)S(1)}, u32[]{:S(2)}, u32[]{:S(2)}) collective-permute-start(f32[136,256]{1,0:T(8,128)S(1)} %get-tuple-element.73), channel_id=1, source_target_pairs={{0,2},{2,4},{4,6},{6,0},{1,3},{3,5},{5,7},{7,1},{8,10},{10,12},{12... | collective-permute-start | bytes 417800 | tf_op jit(solution)/shard_map/ppermute | solution.py:34
  98.5 9.5 %collective-permute-start.22 = (f32[136,256]{1,0:T(8,128)S(1)}, f32[136,256]{1,0:T(8,128)S(1)}, u32[]{:S(2)}, u32[]{:S(2)}) collective-permute-start(f32[136,256]{1,0:T(8,128)S(1)} %get-tuple-element.74), channel_id=1, source_target_pairs={{0,4},{2,6},{4,0},{6,2},{1,5},{3,7},{5,1},{7,3},{8,12},{10,14},{12... | collective-permute-start | bytes 417800 | tf_op jit(solution)/shard_map/ppermute | solution.py:34
  108.9 16.3 %all-to-all-start.1 = ((f32[8,40,256]{2,1,0:T(8,128)}), f32[8,40,256]{2,1,0:T(8,128)S(1)}, u32[]{:S(2)}, u32[]{:S(2)}) async-start(f32[8,40,256]{2,1,0:T(8,128)} %pad_maximum_fusion.4), calls=%async_computation.1 | async-start | bytes 655360 | tf_op jit(solution)/shard_map/all_to_all | solution.py:241
  126.4 2.2 %collective-permute-start.30 = (f32[8,128]{1,0:T(8,128)S(1)}, f32[8,128]{1,0:T(8,128)S(1)}, u32[]{:S(2)}, u32[]{:S(2)}) collective-permute-start(f32[8,128]{1,0:T(8,128)S(1)} %broadcast_in_dim.21), channel_id=1, source_target_pairs={{0,8},{8,0},{1,9},{9,1},{2,10},{10,2},{3,11},{11,3},{4,12},{12,4},... | collective-permute-start | bytes 12296 | tf_op jit(solution)/shard_map/ppermute | solution.py:27
